TPU v7x, 128 devices: a whole 4x4x4 slice. The times are simulated.
128 devices in a mesh: row: 8 (over z_hi, x), col: 16 (over z_lo, y, core).
Axes of the slice: x: 4, y: 4, z: 4 (z_hi: 2, z_lo: 2; z = z_hi * 2 + z_lo), core: 2. Of those that a mesh axis runs over, the one named last changes fastest.
Arguments:
- tokens: bfloat16 [16384, 2048], P(('row', 'col')), may hold values from -6 to 6
- expert_ids: int32 [16384, 8], P(('row', 'col')), may hold values from 0 to 127, all different within a row; in each aligned block of 128 rows (0 to 127, 128 to 255, ...) at most 10 rows name the same one
- gate_probs: float32 [16384, 8], P(('row', 'col')), may hold values from 0.05 to 0.5
- w_gate: bfloat16 [128, 2048, 768], P(('row', 'col')), may hold values from -0.125 to 0.125
- w_up: bfloat16 [128, 2048, 768], P(('row', 'col')), may hold values from -0.125 to 0.125
- w_down: bfloat16 [128, 768, 2048], P(('row', 'col')), may hold values from -0.21875 to 0.21875
Outputs:
- mixed: bfloat16 [16384, 2048], P(('row', 'col'))
Inputs may be any that keep to these rules, and one draw needn't show every extreme that they name: `expert_ids`: each row names 8 different experts; among the rows of one device (aligned blocks of 128 rows) no expert is named more than 10 times.
All inputs are finite; a program needn't handle non-finite values.
Results may differ from a plain program's by a relative error of at most 0.0058.
Values may be sent and summed in bfloat16 or wider, within the bound.
No kernel may reach another device: no remote copies, remote signals or barrier semaphores. Data moves between devices by JAX's collectives and lax.ppermute only.
A program may use at most 128 MiB of HBM per device.

v0:
```python
import jax
import jax.numpy as jnp
from jax import lax
from jax.sharding import PartitionSpec as P


def apply_experts(received, w_gate, w_up, w_down):
    width = received.shape[-1]
    rows = received[:, 0].reshape(-1, width)
    gate = jnp.dot(rows, w_gate[0], preferred_element_type=jnp.float32)
    up = jnp.dot(rows, w_up[0], preferred_element_type=jnp.float32)
    hidden = (jax.nn.silu(gate) * up).astype(jnp.bfloat16)
    result = jnp.dot(hidden, w_down[0], preferred_element_type=jnp.float32).astype(jnp.bfloat16)
    results = [result.reshape(received.shape[0], received.shape[2], width)]
    return jnp.stack(results, axis=1)


def body(tokens, expert_ids, gate_probs, w_gate, w_up, w_down):
    tok_rows, choices_per = expert_ids.shape
    width = tokens.shape[1]
    rows_axis = lax.axis_size("row")
    cols_axis = lax.axis_size("col")
    devices_all = rows_axis * cols_axis
    local_count = w_gate.shape[0]
    expert_count = local_count * devices_all
    slot_count = 5 * tok_rows * choices_per // (4 * expert_count)
    flat_ids = expert_ids.reshape(-1)
    onehot = (flat_ids[:, None] == jnp.arange(expert_count, dtype=jnp.int32)[None, :]).astype(
        jnp.int32
    )
    rank = jnp.sum((jnp.cumsum(onehot, axis=0) - 1) * onehot, axis=1)
    target = flat_ids * slot_count + rank
    repeated = jnp.repeat(tokens, choices_per, axis=0)
    buffer = jnp.zeros((expert_count * slot_count, width), jnp.bfloat16).at[target].set(repeated)
    outgoing = buffer.reshape(devices_all, local_count, slot_count, width)
    produced = apply_experts(
        lax.all_to_all(outgoing, ("row", "col"), split_axis=0, concat_axis=0, tiled=True),
        w_gate,
        w_up,
        w_down,
    )
    returned = lax.all_to_all(produced, ("row", "col"), split_axis=0, concat_axis=0, tiled=True)
    returned = returned.reshape(expert_count * slot_count, width)
    picked = returned[target].reshape(tok_rows, choices_per, width).astype(jnp.float32)
    mixed = jnp.sum(gate_probs[:, :, None] * picked, axis=1)
    return mixed.astype(jnp.bfloat16)


def solution(mesh):
    in_specs = (
        P(("row", "col"), None),
        P(("row", "col"), None),
        P(("row", "col"), None),
        P(("row", "col"), None, None),
        P(("row", "col"), None, None),
        P(("row", "col"), None, None),
    )
    out_specs = P(("row", "col"), None)
    return jax.shard_map(body, mesh=mesh, in_specs=in_specs, out_specs=out_specs, check_vma=False)
```

profile of v0, /device:TPU:3, one launch (start us, length us, event | category | flops | bytes accessed | tf_op | source)
XLA Modules:
  0.0 323.9 jit_solution(10382631951970415099)
XLA Ops:
  0.0 0.0 copy-start
  0.0 0.9 copy.16
  0.9 0.1 eq.29
  1.0 0.1 eq.25
  1.1 0.7 broadcast_multiply_fusion
  1.8 0.1 copy.18
  1.9 0.2 fusion.11
  2.1 0.0 copy-start.3
  2.1 0.8 copy-done.3
  3.0 1.1 add_add_fusion
  4.0 0.9 copy.19
  4.9 0.1 copy.15
  5.0 0.1 mul.37
  5.1 1.4 fusion.10
  6.5 10.1 %scatter_custom_fusion = bf16[1280,2048]{1,0:T(8,128)(2,1)} fusion(s32[1024]{0:T(1024)S(1)} %bitcast.33, bf16[]{:T(256)} %constant.7.clone.1, bf16[128,2048]{1,0:T(8,128)(2,1)} %param.6), kind=kCustom, calls=%fused_computation.5 | custom fusion | bytes 5767170 | tf_op jit(solution)/shard_map/scatter | solution.py:34
  16.7 9.5 %reshape.63 = bf16[128,1,10,2048]{3,2,0,1:T(8,128)(2,1)} reshape(bf16[1280,2048]{1,0:T(8,128)(2,1)} %scatter_custom_fusion) | data formatting | bytes 10485760 | tf_op jit(solution)/shard_map/reshape | solution.py:35
  26.2 114.1 %all_to_all.10 = bf16[128,1,10,2048]{3,2,1,0:T(8,128)(2,1)} all-to-all(bf16[128,1,10,2048]{3,2,1,0:T(8,128)(2,1)} %bitcast.31), channel_id=1, replica_groups=mesh['row'=8,'col'=16] {'row','col'}, dimensions={0} | all-to-all | bytes 10485760 | tf_op jit(solution)/shard_map/all_to_all | solution.py:37
  140.3 9.8 %reshape_squeeze.3 = bf16[1280,2048]{1,0:T(8,128)(2,1)} reshape(bf16[128,1,10,2048]{3,2,1,0:T(8,128)(2,1)} %all_to_all.10) | data formatting | bytes 10485760 | tf_op jit(solution)/shard_map/reshape;squeeze | solution.py:9
  150.2 0.0 copy-start.2
  150.2 0.0 copy-start.5
  150.2 7.2 %fusion.6 = f32[1280,768]{1,0:T(8,128)S(1)} fusion(bf16[1280,2048]{1,0:T(8,128)(2,1)} %reshape_squeeze.3, bf16[1,2048,768]{2,1,0:T(8,128)(2,1)} %param.9), kind=kOutput, calls=%fused_computation.11 | convolution fusion | flops 4026531840 | bytes 12320768 | tf_op jit(solution)/shard_map/dot_general | solution.py:10
  157.4 0.0 copy-done.2
  157.4 0.0 copy-done.5
  157.4 4.8 %fusion.3 = bf16[1280,768]{1,0:T(8,128)(2,1)S(1)} fusion(bf16[1280,2048]{1,0:T(8,128)(2,1)S(1)} %copy-done.2, f32[1280,768]{1,0:T(8,128)S(1)} %fusion.6, bf16[1,2048,768]{2,1,0:T(8,128)(2,1)S(1)} %copy-done.5), kind=kOutput, calls=%fused_computation.8 | convolution fusion | flops 4032430080 | bytes 14286848 | tf_op jit(solution)/shard_map/dot_general | solution.py:11
  162.2 0.0 copy-done
  162.2 6.0 %convolution_convert_fusion = bf16[1280,2048]{1,0:T(8,128)(2,1)} fusion(bf16[1280,768]{1,0:T(8,128)(2,1)S(1)} %fusion.3, bf16[1,768,2048]{2,1,0:T(8,128)(2,1)S(1)} %copy-done), kind=kOutput, calls=%fused_computation.4 | convolution fusion | flops 4029153280 | bytes 10354688 | tf_op jit(solution)/shard_map/dot_general | solution.py:13
  168.3 9.5 %stack_reshape.3 = bf16[128,1,10,2048]{3,2,0,1:T(8,128)(2,1)} reshape(bf16[1280,2048]{1,0:T(8,128)(2,1)} %convolution_convert_fusion) | data formatting | bytes 10485760 | tf_op jit(solution)/shard_map/stack;reshape | solution.py:15
  177.8 0.0 copy-start.4
  177.8 11.1 %all-to-all-start.1 = ((bf16[128,1,10,2048]{3,2,1,0:T(8,128)(2,1)}), bf16[128,1,10,2048]{3,2,1,0:T(8,128)(2,1)}, u32[]{:S(2)}, u32[]{:S(2)}) async-start(bf16[128,1,10,2048]{3,2,1,0:T(8,128)(2,1)} %bitcast.30), calls=%async_computation.1 | async-start | bytes 16777216 | tf_op jit(solution)/shard_map/all_to_all | solution.py:42
  189.0 0.0 copy-done.4
  189.0 0.1 copy.14
  189.1 105.5 %all-to-all-done.1 = bf16[128,1,10,2048]{3,2,1,0:T(8,128)(2,1)} async-done(((bf16[128,1,10,2048]{3,2,1,0:T(8,128)(2,1)}), bf16[128,1,10,2048]{3,2,1,0:T(8,128)(2,1)}, u32[]{:S(2)}, u32[]{:S(2)}) %all-to-all-start.1) | async-done | bytes 5242912 | tf_op jit(solution)/shard_map/all_to_all | solution.py:42
  294.6 9.8 %reshape.64 = bf16[1280,2048]{1,0:T(8,128)(2,1)} reshape(bf16[128,1,10,2048]{3,2,1,0:T(8,128)(2,1)} %all-to-all-done.1) | data formatting | bytes 10485760 | tf_op jit(solution)/shard_map/reshape | solution.py:43
  304.4 0.0 copy-start.1
  304.4 12.1 %gather_fusion = bf16[1024,2048]{1,0:T(8,128)(2,1)} fusion(bf16[1280,2048]{1,0:T(8,128)(2,1)} %reshape.64, s32[1024]{0:T(1024)S(1)} %broadcast_clamp_fusion), kind=kCustom, calls=%fused_computation | custom fusion | bytes 8392704 | tf_op jit(solution)/shard_map/gather | solution.py:44
  316.6 7.3 %fusion = bf16[128,2048]{1,0:T(8,128)(2,1)} fusion(bf16[1024,2048]{1,0:T(8,128)(2,1)} %gather_fusion, f32[128,8]{1,0:T(8,128)S(1)} %copy.14), kind=kLoop, calls=%fused_computation.3 | loop fusion | flops 6029312 | bytes 4722688 | tf_op jit(solution)/shard_map/reduce_sum | solution.py:45
  323.9 0.0 copy-done.1
  (5 shorter events, 0.0 us)
Async XLA Ops:
  0.0 162.2 %copy-start = (bf16[1,768,2048]{2,1,0:T(8,128)(2,1)S(1)}, bf16[1,768,2048]{2,1,0:T(8,128)(2,1)}, u32[]{:S(2)}) copy-start(bf16[1,768,2048]{2,1,0:T(8,128)(2,1)} %param.11) | copy-start | bytes 9437188
  2.1 0.8 copy-start.3
  150.2 7.3 %copy-start.2 = (bf16[1280,2048]{1,0:T(8,128)(2,1)S(1)}, bf16[1280,2048]{1,0:T(8,128)(2,1)}, u32[]{:S(2)}) copy-start(bf16[1280,2048]{1,0:T(8,128)(2,1)} %reshape_squeeze.3) | copy-start | bytes 15728644
  150.2 7.3 %copy-start.5 = (bf16[1,2048,768]{2,1,0:T(8,128)(2,1)S(1)}, bf16[1,2048,768]{2,1,0:T(8,128)(2,1)}, u32[]{:S(2)}) copy-start(bf16[1,2048,768]{2,1,0:T(8,128)(2,1)} %param.10) | copy-start | bytes 9437188
  177.8 11.2 %copy-start.4 = (f32[128,8]{0,1:T(8,128)S(1)}, f32[128,8]{0,1:T(8,128)}, u32[]{:S(2)}) copy-start(f32[128,8]{0,1:T(8,128)} %param.8) | copy-start | bytes 12292
  177.8 116.8 %all-to-all-start.1 = ((bf16[128,1,10,2048]{3,2,1,0:T(8,128)(2,1)}), bf16[128,1,10,2048]{3,2,1,0:T(8,128)(2,1)}, u32[]{:S(2)}, u32[]{:S(2)}) async-start(bf16[128,1,10,2048]{3,2,1,0:T(8,128)(2,1)} %bitcast.30), calls=%async_computation.1 | async-start | bytes 16777216 | tf_op jit(solution)/shard_map/all_to_all | solution.py:42
  304.4 19.5 %copy-start.1 = (bf16[1,768,2048]{2,1,0:T(8,128)(2,1)S(1)}, bf16[1,768,2048]{2,1,0:T(8,128)(2,1)}, u32[]{:S(2)}) copy-start(bf16[1,768,2048]{2,1,0:T(8,128)(2,1)} %param.11) | copy-start | bytes 9437188
where the time goes:
time: 330 us; the launch traced here: 324 us
  blocking collectives  114 us (35%)
  waiting for transfers between devices  105 us (32%)
  local copies, waits for them, and re-layouts  64.3 us (19%)
  matrix products  18.1 us (5%)
  starting transfers between devices  11.1 us (3%)
  other arithmetic  10.7 us (3%)
    all_to_all x1, blocking collectives, body(): lax.all_to_all(outgoing, ('row', 'col'), split_axis=0, concat_axis=0, til...  114 us
    all_to_all x1, waiting for transfers between devices, body(): lax.all_to_all(produced, ('row', 'col'), split_axis=0, concat_axis=0, til...  105 us
    gather x1, local copies, waits for them, and re-layouts, body(): returned[target].reshape(tok_rows, choices_per, width).astype(jnp.float32)  12.1 us
    all_to_all x1, starting transfers between devices, body(): lax.all_to_all(produced, ('row', 'col'), split_axis=0, concat_axis=0, til...  11.1 us
    scatter x1, local copies, waits for them, and re-layouts, body(): jnp.zeros((expert_count * slot_count, width), jnp.bfloat16).at[target]  10.1 us
    another operation x1, local copies, waits for them, and re-layouts, apply_experts(): rows = received[:, 0].reshape(-1, width)  9.85 us
    reshape x1, local copies, waits for them, and re-layouts, body(): returned = returned.reshape(expert_count * slot_count, width)  9.84 us
    reshape x1, local copies, waits for them, and re-layouts, body(): outgoing = buffer.reshape(devices_all, local_count, slot_count, width)  9.54 us
  transfers between devices with their start and end apart: 1, of which 1 were waited for; matrix products, arithmetic and copies ran while one was open for 0% of the time, Pallas kernels for 0%

commit v1 on v0

v1 whole, which is shorter than its diff:
```python
import functools

import jax
import jax.numpy as jnp
from jax import lax
from jax.experimental import pallas as pl
from jax.experimental.pallas import tpu as pltpu
from jax.sharding import PartitionSpec as P

BF = jnp.bfloat16
F32 = jnp.float32
LANES = 128
SUB = 16


def swap_matrix():
    i = lax.broadcasted_iota(jnp.int32, (SUB * SUB, SUB * SUB), 0)
    j = lax.broadcasted_iota(jnp.int32, (SUB * SUB, SUB * SUB), 1)
    return (j == (i % SUB) * SUB + i // SUB).astype(F32).astype(BF)


def dispatch_kernel(slots, ids_ref, tok_ref, out_ref, pos_ref, tiles, pos_smem, sem):
    top, rows = ids_ref.shape
    experts = out_ref.shape[0] // slots
    ids = ids_ref[...]
    expert = lax.broadcasted_iota(jnp.int32, (experts, rows), 0)
    named = jnp.zeros((experts, rows), F32)
    for k in range(top):
        named += (ids[k : k + 1, :] == expert).astype(F32)
    before = lax.broadcasted_iota(jnp.int32, (rows, rows), 0)
    after = lax.broadcasted_iota(jnp.int32, (rows, rows), 1)
    earlier = (before < after).astype(F32).astype(BF)
    rank = jnp.dot(named.astype(BF), earlier, preferred_element_type=F32)
    slot = expert.astype(F32) * slots + rank
    for k in range(top):
        mine = jnp.where(ids[k : k + 1, :] == expert, slot, 0.0)
        pos_ref[k : k + 1, :] = jnp.sum(mine, axis=0, keepdims=True).astype(jnp.int32)
    copy = pltpu.make_async_copy(pos_ref, pos_smem, sem)
    copy.start()

    swap = swap_matrix()
    for b in range(rows // (2 * SUB)):
        halves = []
        for h in range(2):
            at = (2 * b + h) * SUB
            halves.append(
                jnp.concatenate(
                    [tok_ref[at : at + SUB, c * LANES : (c + 1) * LANES] for c in range(SUB)], axis=0
                )
            )
        moved = jnp.dot(swap, jnp.concatenate(halves, axis=1), preferred_element_type=F32).astype(BF)
        for h in range(2):
            at = (2 * b + h) * SUB
            tiles[at : at + SUB] = moved[:, h * LANES : (h + 1) * LANES].reshape(SUB, SUB, LANES)

    def clear(i, _):
        for j in range(slots):
            out_ref[i * slots + j] = jnp.zeros((SUB, LANES), BF)
        return 0

    lax.fori_loop(0, experts, clear, 0)
    copy.wait()

    def place(t, _):
        tile = tiles[t]
        for k in range(top):
            out_ref[pos_smem[k, t]] = tile
        return 0

    lax.fori_loop(0, rows, place, 0)


def ffn_kernel(x_ref, wg_ref, wu_ref, wd_ref, out_ref, rows_ref):
    swap = swap_matrix()
    rows = rows_ref.shape[0]
    for b in range(rows // (2 * SUB)):
        lo = x_ref[(2 * b) * 256 : (2 * b + 1) * 256, :]
        hi = x_ref[(2 * b + 1) * 256 : (2 * b + 2) * 256, :]
        moved = jnp.dot(swap, jnp.concatenate([lo, hi], axis=1), preferred_element_type=F32).astype(BF)
        for h in range(2):
            for c in range(SUB):
                rows_ref[(2 * b + h) * SUB : (2 * b + h + 1) * SUB, c * LANES : (c + 1) * LANES] = moved[
                    c * SUB : (c + 1) * SUB, h * LANES : (h + 1) * LANES
                ]
    x = rows_ref[...]
    gate = jnp.dot(x, wg_ref[...], preferred_element_type=F32)
    up = jnp.dot(x, wu_ref[...], preferred_element_type=F32)
    hidden = (gate / (1.0 + jnp.exp(-gate)) * up).astype(BF)
    rows_ref[...] = jnp.dot(hidden, wd_ref[...], preferred_element_type=F32).astype(BF)
    for b in range(rows // (2 * SUB)):
        halves = []
        for h in range(2):
            at = (2 * b + h) * SUB
            halves.append(
                jnp.concatenate(
                    [rows_ref[at : at + SUB, c * LANES : (c + 1) * LANES] for c in range(SUB)], axis=0
                )
            )
        moved = jnp.dot(swap, jnp.concatenate(halves, axis=1), preferred_element_type=F32).astype(BF)
        for h in range(2):
            out_ref[(2 * b + h) * 256 : (2 * b + h + 1) * 256, :] = moved[:, h * LANES : (h + 1) * LANES]


def combine_kernel(pos_ref, prob_ref, x_ref, out_ref, tiles):
    top, rows = pos_ref.shape

    def mix(t, _):
        total = jnp.zeros((SUB, LANES), F32)
        for k in range(top):
            total += prob_ref[k, t] * x_ref[pos_ref[k, t]].astype(F32)
        tiles[t] = total.astype(BF)
        return 0

    lax.fori_loop(0, rows, mix, 0)
    swap = swap_matrix()
    for b in range(rows // (2 * SUB)):
        halves = []
        for h in range(2):
            at = (2 * b + h) * SUB
            halves.append(tiles[at : at + SUB].reshape(SUB * SUB, LANES))
        moved = jnp.dot(swap, jnp.concatenate(halves, axis=1), preferred_element_type=F32).astype(BF)
        for h in range(2):
            at = (2 * b + h) * SUB
            for c in range(SUB):
                out_ref[at : at + SUB, c * LANES : (c + 1) * LANES] = moved[
                    c * SUB : (c + 1) * SUB, h * LANES : (h + 1) * LANES
                ]


def body(tokens, expert_ids, gate_probs, w_gate, w_up, w_down):
    rows, top = expert_ids.shape
    width = tokens.shape[1]
    hidden = w_gate.shape[2]
    experts = lax.axis_size("row") * lax.axis_size("col")
    slots = 5 * rows * top // (4 * experts)
    total = experts * slots
    vmem = pl.BlockSpec(memory_space=pltpu.VMEM)
    smem = pl.BlockSpec(memory_space=pltpu.SMEM)
    limit = pltpu.CompilerParams(vmem_limit_bytes=56 * 1024 * 1024)

    buffer, pos = pl.pallas_call(
        functools.partial(dispatch_kernel, slots),
        out_shape=(
            jax.ShapeDtypeStruct((total, SUB, LANES), BF),
            jax.ShapeDtypeStruct((top, rows), jnp.int32),
        ),
        in_specs=[vmem, vmem],
        out_specs=(vmem, vmem),
        scratch_shapes=[
            pltpu.VMEM((rows, SUB, LANES), BF),
            pltpu.SMEM((top, rows), jnp.int32),
            pltpu.SemaphoreType.DMA,
        ],
        compiler_params=limit,
        name="dispatch",
    )(expert_ids.T, tokens)

    wire = buffer.reshape(experts, slots * SUB, LANES)
    wire = lax.all_to_all(wire, ("row", "col"), split_axis=0, concat_axis=0, tiled=True)

    step = 256
    whole = lambda i: (0, 0)
    wire = pl.pallas_call(
        ffn_kernel,
        grid=(total // step,),
        out_shape=jax.ShapeDtypeStruct((total * SUB, LANES), BF),
        in_specs=[
            pl.BlockSpec((step * SUB, LANES), lambda i: (i, 0)),
            pl.BlockSpec((width, hidden), whole),
            pl.BlockSpec((width, hidden), whole),
            pl.BlockSpec((hidden, width), whole),
        ],
        out_specs=pl.BlockSpec((step * SUB, LANES), lambda i: (i, 0)),
        scratch_shapes=[pltpu.VMEM((step, width), BF)],
        compiler_params=limit,
        name="ffn",
    )(wire.reshape(total * SUB, LANES), w_gate[0], w_up[0], w_down[0])

    wire = wire.reshape(experts, slots * SUB, LANES)
    wire = lax.all_to_all(wire, ("row", "col"), split_axis=0, concat_axis=0, tiled=True)

    return pl.pallas_call(
        combine_kernel,
        out_shape=jax.ShapeDtypeStruct((rows, width), BF),
        in_specs=[smem, smem, vmem],
        out_specs=vmem,
        scratch_shapes=[pltpu.VMEM((rows, SUB, LANES), BF)],
        compiler_params=limit,
        name="combine",
    )(pos, gate_probs.T, wire.reshape(total, SUB, LANES))


def solution(mesh):
    in_specs = (
        P(("row", "col"), None),
        P(("row", "col"), None),
        P(("row", "col"), None),
        P(("row", "col"), None, None),
        P(("row", "col"), None, None),
        P(("row", "col"), None, None),
    )
    out_specs = P(("row", "col"), None)
    return jax.shard_map(body, mesh=mesh, in_specs=in_specs, out_specs=out_specs, check_vma=False)
```

time: 330 us -> 184 us (0.56); the launches traced: 324 us -> 184 us
  waiting for transfers between devices: 105 us -> 0 us
  local copies, waits for them, and re-layouts: 64.3 us -> 0 us
  blocking collectives: 114 us -> 149 us
  Pallas kernels: 0 us -> 34.7 us
  matrix products: 18.1 us -> 0 us
  starting transfers between devices: 11.1 us -> 0 us
  other arithmetic: 10.7 us -> 0 us
    all_to_all x1 -> x0, waiting for transfers between devices: 105 us -> none  [body(): lax.all_to_all(produced, ('row', 'col'), split_axis=0, concat_axis=0, til...]
    all_to_all x1 -> x2, blocking collectives: 114 us -> 149 us  [body(): lax.all_to_all(wire, ('row', 'col'), split_axis=0, concat_axis=0, tiled=T...]
    pallas_call x0 -> x3, Pallas kernels: none -> 34.7 us  [the longest x1 21.6 us: body(): pl.pallas_call(ffn_kernel, grid=(total // step,), out_shape=jax.ShapeDtyp...]
    reshape x2 -> x0, local copies, waits for them, and re-layouts: 19.4 us -> none  [the longest x1 9.84 us: body(): returned = returned.reshape(expert_count * slot_count, width)]
    another operation x4 -> x0, local copies, waits for them, and re-layouts: 19.4 us -> none  [the longest x1 9.85 us: apply_experts(): rows = received[:, 0].reshape(-1, width)]
    dot_general x3 -> x0, matrix products: 18.1 us -> none  [the longest x1 7.24 us: apply_experts(): gate = jnp.dot(rows, w_gate[0], preferred_element_type=jnp.float32)]
    gather x1 -> x0, local copies, waits for them, and re-layouts: 12.1 us -> none  [body(): returned[target].reshape(tok_rows, choices_per, width).astype(jnp.float32)]
    all_to_all x1 -> x0, starting transfers between devices: 11.1 us -> none  [body(): lax.all_to_all(produced, ('row', 'col'), split_axis=0, concat_axis=0, til...]
  transfers between devices with their start and end apart: 1 -> 0, of which waited for: 1 -> 0; matrix products, arithmetic and copies ran while one was open for 0% -> 0% of each run, Pallas kernels for 0% -> 0%
where the time goes in v1:
time: 184 us
  blocking collectives  149 us (81%)
  Pallas kernels  34.7 us (19%)
    all_to_all x2, blocking collectives, body(): lax.all_to_all(wire, ('row', 'col'), split_axis=0, concat_axis=0, tiled=T...  149 us
    pallas_call x1, Pallas kernels, body(): pl.pallas_call(ffn_kernel, grid=(total // step,), out_shape=jax.ShapeDtyp...  21.6 us
    pallas_call x1, Pallas kernels, body(): pl.pallas_call(functools.partial(dispatch_kernel, slots), out_shape=(jax....  6.8 us
    pallas_call x1, Pallas kernels, body(): pl.pallas_call(combine_kernel, out_shape=jax.ShapeDtypeStruct((rows, widt...  6.36 us

profile of v1, /device:TPU:3, one launch (start us, length us, event | category | flops | bytes accessed | tf_op | source)
XLA Modules:
  0.0 184.1 jit_solution(6044964568882499142)
XLA Ops:
  0.0 6.8 %dispatch.1 = (bf16[1280,16,128]{2,1,0:T(8,128)(2,1)}, s32[8,128]{1,0:T(8,128)}) custom-call(s32[8,128]{1,0:T(8,128)} %bitcast.16, bf16[128,2048]{1,0:T(8,128)(2,1)} %tok_ref.1), custom_call_target="tpu_custom_call" | custom-call | tf_op jit(solution)/shard_map/dispatch/pallas_call | solution.py:141
  6.8 76.5 %all_to_all.10 = bf16[128,160,128]{2,1,0:T(8,128)(2,1)} all-to-all(bf16[128,160,128]{2,1,0:T(8,128)(2,1)} %bitcast.12), channel_id=1, replica_groups=mesh['row'=8,'col'=16] {'row','col'}, dimensions={0} | all-to-all | bytes 10485760 | tf_op jit(solution)/shard_map/all_to_all | solution.py:159
  83.3 21.6 %ffn.1 = bf16[20480,128]{1,0:T(8,128)(2,1)} custom-call(bf16[20480,128]{1,0:T(8,128)(2,1)} %bitcast.10, bf16[2048,768]{1,0:T(8,128)(2,1)} %bitcast.13, bf16[2048,768]{1,0:T(8,128)(2,1)} %bitcast.14, bf16[768,2048]{1,0:T(8,128)(2,1)} %bitcast.15), custom_call_target="tpu_custom_call" | custom-call | tf_op jit(solution)/shard_map/ffn/pallas_call | solution.py:163
  104.9 72.8 %all_to_all.11 = bf16[128,160,128]{2,1,0:T(8,128)(2,1)} all-to-all(bf16[128,160,128]{2,1,0:T(8,128)(2,1)} %bitcast.11), channel_id=1, replica_groups=mesh['row'=8,'col'=16] {'row','col'}, dimensions={0} | all-to-all | bytes 10485760 | tf_op jit(solution)/shard_map/all_to_all | solution.py:180
  177.7 6.4 %combine.1 = bf16[128,2048]{1,0:T(8,128)(2,1)} custom-call(s32[8,128]{1,0:T(8,128)} %get-tuple-element.7.pos_ref, f32[8,128]{1,0:T(8,128)} %bitcast.17, bf16[1280,16,128]{2,1,0:T(8,128)(2,1)} %bitcast.9), custom_call_target="tpu_custom_call" | custom-call | tf_op jit(solution)/shard_map/combine/pallas_call | solution.py:182

commit v2 on v1

--- a/solution.py
+++ b/solution.py
@@ -136,7 +136,7 @@
     total = experts * slots
     vmem = pl.BlockSpec(memory_space=pltpu.VMEM)
     smem = pl.BlockSpec(memory_space=pltpu.SMEM)
-    limit = pltpu.CompilerParams(vmem_limit_bytes=56 * 1024 * 1024)
+    limit = pltpu.CompilerParams(vmem_limit_bytes=32 * 1024 * 1024)
 
     buffer, pos = pl.pallas_call(
         functools.partial(dispatch_kernel, slots),

time: 184 us -> 175 us (0.951)
  Pallas kernels: 34.7 us -> 24.4 us
    pallas_call x1, Pallas kernels: 21.6 us -> 16.5 us  [body(): pl.pallas_call(ffn_kernel, grid=(total // step,), out_shape=jax.ShapeDtyp...]
    pallas_call x1, Pallas kernels: 6.8 us -> 3.36 us  [body(): pl.pallas_call(functools.partial(dispatch_kernel, slots), out_shape=(jax....]
where the time goes in v2:
time: 175 us
  blocking collectives  149 us (85%)
  Pallas kernels  24.4 us (14%)
  local copies, waits for them, and re-layouts  1.75 us (1%)
    all_to_all x2, blocking collectives, body(): lax.all_to_all(wire, ('row', 'col'), split_axis=0, concat_axis=0, tiled=T...  149 us
    pallas_call x1, Pallas kernels, body(): pl.pallas_call(ffn_kernel, grid=(total // step,), out_shape=jax.ShapeDtyp...  16.5 us
    pallas_call x1, Pallas kernels, body(): pl.pallas_call(combine_kernel, out_shape=jax.ShapeDtypeStruct((rows, widt...  4.52 us

profile of v2, /device:TPU:3, one launch (start us, length us, event | category | flops | bytes accessed | tf_op | source)
XLA Modules:
  0.0 175.0 jit_solution(12117021872257770312)
XLA Ops:
  0.0 0.0 copy-start.3
  0.0 1.0 copy-done.3
  1.0 0.0 copy-start.4
  1.0 0.7 copy-done.4
  1.7 3.4 %dispatch.1 = (bf16[1280,16,128]{2,1,0:T(8,128)(2,1)S(1)}, s32[8,128]{1,0:T(8,128)S(1)}) custom-call(s32[8,128]{1,0:T(8,128)S(1)} %bitcast.16, bf16[128,2048]{1,0:T(8,128)(2,1)S(1)} %copy-done.3), custom_call_target="tpu_custom_call" | custom-call | tf_op jit(solution)/shard_map/dispatch/pallas_call | solution.py:141
  5.1 0.0 copy-start
  5.1 0.0 copy-start.1
  5.1 0.0 copy-start.2
  5.1 76.2 %all_to_all.10 = bf16[128,160,128]{2,1,0:T(8,128)(2,1)S(1)} all-to-all(bf16[128,160,128]{2,1,0:T(8,128)(2,1)S(1)} %bitcast.12), channel_id=1, replica_groups=mesh['row'=8,'col'=16] {'row','col'}, dimensions={0} | all-to-all | bytes 10485760 | tf_op jit(solution)/shard_map/all_to_all | solution.py:159
  81.3 0.0 copy-done
  81.4 0.0 copy-done.1
  81.4 0.0 copy-done.2
  81.4 16.5 %ffn.1 = bf16[20480,128]{1,0:T(8,128)(2,1)S(1)} custom-call(bf16[20480,128]{1,0:T(8,128)(2,1)S(1)} %bitcast.10, bf16[2048,768]{1,0:T(8,128)(2,1)S(1)} %bitcast.13, bf16[2048,768]{1,0:T(8,128)(2,1)S(1)} %bitcast.14, bf16[768,2048]{1,0:T(8,128)(2,1)S(1)} %bitcast.15), custom_call_target="tpu_custom_call" | custom-call | tf_op jit(solution)/shard_map/ffn/pallas_call | solution.py:163
  97.9 0.0 copy-start.5
  97.9 72.5 %all_to_all.11 = bf16[128,160,128]{2,1,0:T(8,128)(2,1)S(1)} all-to-all(bf16[128,160,128]{2,1,0:T(8,128)(2,1)S(1)} %bitcast.11), channel_id=1, replica_groups=mesh['row'=8,'col'=16] {'row','col'}, dimensions={0} | all-to-all | bytes 10485760 | tf_op jit(solution)/shard_map/all_to_all | solution.py:180
  170.4 0.0 copy-done.5
  170.4 4.5 %combine.1 = bf16[128,2048]{1,0:T(8,128)(2,1)} custom-call(s32[8,128]{1,0:T(8,128)S(1)} %get-tuple-element.7.pos_ref, f32[8,128]{1,0:T(8,128)S(1)} %bitcast.17, bf16[1280,16,128]{2,1,0:T(8,128)(2,1)S(1)} %bitcast.9), custom_call_target="tpu_custom_call" | custom-call | tf_op jit(solution)/shard_map/combine/pallas_call | solution.py:182
Async XLA Ops:
  0.0 1.0 copy-start.3
  1.0 0.7 copy-start.4
  5.1 76.2 %copy-start = (bf16[1,2048,768]{2,1,0:T(8,128)(2,1)S(1)}, bf16[1,2048,768]{2,1,0:T(8,128)(2,1)}, u32[]{:S(2)}) copy-start(bf16[1,2048,768]{2,1,0:T(8,128)(2,1)} %param.9) | copy-start | bytes 9437188
  5.1 76.2 %copy-start.1 = (bf16[1,2048,768]{2,1,0:T(8,128)(2,1)S(1)}, bf16[1,2048,768]{2,1,0:T(8,128)(2,1)}, u32[]{:S(2)}) copy-start(bf16[1,2048,768]{2,1,0:T(8,128)(2,1)} %param.10) | copy-start | bytes 9437188
  5.1 76.2 %copy-start.2 = (bf16[1,768,2048]{2,1,0:T(8,128)(2,1)S(1)}, bf16[1,768,2048]{2,1,0:T(8,128)(2,1)}, u32[]{:S(2)}) copy-start(bf16[1,768,2048]{2,1,0:T(8,128)(2,1)} %param.11) | copy-start | bytes 9437188
  97.9 72.5 %copy-start.5 = (f32[128,8]{0,1:T(8,128)S(1)}, f32[128,8]{0,1:T(8,128)}, u32[]{:S(2)}) copy-start(f32[128,8]{0,1:T(8,128)} %param.8) | copy-start | bytes 12292

commit v3 on v2

v3 whole, which is shorter than its diff:
```python
import functools

import jax
import jax.numpy as jnp
from jax import lax
from jax.experimental import pallas as pl
from jax.experimental.pallas import tpu as pltpu
from jax.sharding import PartitionSpec as P

BF = jnp.bfloat16
F32 = jnp.float32
LANES = 128
SUB = 16


def swap_matrix():
    i = lax.broadcasted_iota(jnp.int32, (SUB * SUB, SUB * SUB), 0)
    j = lax.broadcasted_iota(jnp.int32, (SUB * SUB, SUB * SUB), 1)
    return (j == (i % SUB) * SUB + i // SUB).astype(F32).astype(BF)


def dispatch_kernel(slots, ids_hbm, tok_hbm, out_ref, pos_ref, ids_ref, tok_ref, tiles, pos_smem, sems):
    top, rows = ids_ref.shape
    experts = out_ref.shape[0] // slots
    get_ids = pltpu.make_async_copy(ids_hbm, ids_ref, sems.at[0])
    get_tok = pltpu.make_async_copy(tok_hbm, tok_ref, sems.at[1])
    get_ids.start()
    get_tok.start()

    def clear(i, _):
        for j in range(4 * slots):
            out_ref[i * (4 * slots) + j] = jnp.zeros((SUB, LANES), BF)
        return 0

    lax.fori_loop(0, experts // 4, clear, 0)
    get_ids.wait()
    ids = ids_ref[...]
    expert = lax.broadcasted_iota(jnp.int32, (experts, rows), 0)
    named = jnp.zeros((experts, rows), F32)
    for k in range(top):
        named += (ids[k : k + 1, :] == expert).astype(F32)
    before = lax.broadcasted_iota(jnp.int32, (rows, rows), 0)
    after = lax.broadcasted_iota(jnp.int32, (rows, rows), 1)
    earlier = (before < after).astype(F32).astype(BF)
    rank = jnp.dot(named.astype(BF), earlier, preferred_element_type=F32)
    slot = expert.astype(F32) * slots + rank
    for k in range(top):
        mine = jnp.where(ids[k : k + 1, :] == expert, slot, 0.0)
        pos_ref[k : k + 1, :] = jnp.sum(mine, axis=0, keepdims=True).astype(jnp.int32)
    to_smem = pltpu.make_async_copy(pos_ref, pos_smem, sems.at[2])
    to_smem.start()

    get_tok.wait()
    swap = swap_matrix()
    for b in range(rows // (2 * SUB)):
        halves = []
        for h in range(2):
            at = (2 * b + h) * SUB
            halves.append(
                jnp.concatenate(
                    [tok_ref[at : at + SUB, c * LANES : (c + 1) * LANES] for c in range(SUB)], axis=0
                )
            )
        moved = jnp.dot(swap, jnp.concatenate(halves, axis=1), preferred_element_type=F32).astype(BF)
        for h in range(2):
            at = (2 * b + h) * SUB
            tiles[at : at + SUB] = moved[:, h * LANES : (h + 1) * LANES].reshape(SUB, SUB, LANES)
    to_smem.wait()

    def place(i, _):
        for j in range(4):
            t = i * 4 + j
            tile = tiles[t]
            for k in range(top):
                out_ref[pos_smem[k, t]] = tile
        return 0

    lax.fori_loop(0, rows // 4, place, 0)


def ffn_kernel(step, x_ref, wg_ref, wu_ref, wd_ref, out_ref, rows_ref):
    swap = swap_matrix()
    rows = step

    def block(i, _):
        base = i * (rows * SUB)
        for b in range(rows // (2 * SUB)):
            lo = x_ref[pl.ds(base + (2 * b) * 256, 256), :]
            hi = x_ref[pl.ds(base + (2 * b + 1) * 256, 256), :]
            moved = jnp.dot(swap, jnp.concatenate([lo, hi], axis=1), preferred_element_type=F32).astype(BF)
            for h in range(2):
                for c in range(SUB):
                    rows_ref[(2 * b + h) * SUB : (2 * b + h + 1) * SUB, c * LANES : (c + 1) * LANES] = moved[
                        c * SUB : (c + 1) * SUB, h * LANES : (h + 1) * LANES
                    ]
        x = rows_ref[...]
        gate = jnp.dot(x, wg_ref[...], preferred_element_type=F32)
        up = jnp.dot(x, wu_ref[...], preferred_element_type=F32)
        hidden = (gate / (1.0 + jnp.exp(-gate)) * up).astype(BF)
        rows_ref[...] = jnp.dot(hidden, wd_ref[...], preferred_element_type=F32).astype(BF)
        for b in range(rows // (2 * SUB)):
            halves = []
            for h in range(2):
                at = (2 * b + h) * SUB
                halves.append(
                    jnp.concatenate(
                        [rows_ref[at : at + SUB, c * LANES : (c + 1) * LANES] for c in range(SUB)], axis=0
                    )
                )
            moved = jnp.dot(swap, jnp.concatenate(halves, axis=1), preferred_element_type=F32).astype(BF)
            for h in range(2):
                out_ref[pl.ds(base + (2 * b + h) * 256, 256), :] = moved[:, h * LANES : (h + 1) * LANES]
        return 0

    lax.fori_loop(0, x_ref.shape[0] // (rows * SUB), block, 0)


def combine_kernel(pos_ref, prob_ref, x_ref, out_hbm, tiles, out_ref, sems):
    top, rows = pos_ref.shape
    swap = swap_matrix()
    part = 2 * SUB
    copies = []
    for b in range(rows // part):

        def mix(i, _):
            for j in range(4):
                t = i * 4 + j
                total = prob_ref[0, b * part + t] * x_ref[pos_ref[0, b * part + t]].astype(F32)
                for k in range(1, top):
                    total += prob_ref[k, b * part + t] * x_ref[pos_ref[k, b * part + t]].astype(F32)
                tiles[t] = total.astype(BF)
            return 0

        lax.fori_loop(0, part // 4, mix, 0)
        halves = [tiles[h * SUB : (h + 1) * SUB].reshape(SUB * SUB, LANES) for h in range(2)]
        moved = jnp.dot(swap, jnp.concatenate(halves, axis=1), preferred_element_type=F32).astype(BF)
        for h in range(2):
            at = (2 * b + h) * SUB
            for c in range(SUB):
                out_ref[at : at + SUB, c * LANES : (c + 1) * LANES] = moved[
                    c * SUB : (c + 1) * SUB, h * LANES : (h + 1) * LANES
                ]
        put = pltpu.make_async_copy(
            out_ref.at[pl.ds(b * part, part), :], out_hbm.at[pl.ds(b * part, part), :], sems.at[b]
        )
        put.start()
        copies.append(put)
    for put in copies:
        put.wait()


def in_hbm(x):
    return pltpu.with_memory_space_constraint(x, pltpu.HBM)


def body(tokens, expert_ids, gate_probs, w_gate, w_up, w_down):
    rows, top = expert_ids.shape
    width = tokens.shape[1]
    hidden = w_gate.shape[2]
    experts = lax.axis_size("row") * lax.axis_size("col")
    slots = 5 * rows * top // (4 * experts)
    total = experts * slots
    vmem = pl.BlockSpec(memory_space=pltpu.VMEM)
    smem = pl.BlockSpec(memory_space=pltpu.SMEM)
    hbm = pl.BlockSpec(memory_space=pltpu.HBM)
    limit = pltpu.CompilerParams(vmem_limit_bytes=32 * 1024 * 1024)

    buffer, pos = pl.pallas_call(
        functools.partial(dispatch_kernel, slots),
        out_shape=(
            jax.ShapeDtypeStruct((total, SUB, LANES), BF),
            jax.ShapeDtypeStruct((top, rows), jnp.int32),
        ),
        in_specs=[hbm, hbm],
        out_specs=(vmem, vmem),
        scratch_shapes=[
            pltpu.VMEM((top, rows), jnp.int32),
            pltpu.VMEM((rows, width), BF),
            pltpu.VMEM((rows, SUB, LANES), BF),
            pltpu.SMEM((top, rows), jnp.int32),
            pltpu.SemaphoreType.DMA((3,)),
        ],
        compiler_params=limit,
        name="dispatch",
    )(in_hbm(expert_ids.T), in_hbm(tokens))

    wire = buffer.reshape(experts, slots * SUB, LANES)
    wire = lax.all_to_all(wire, ("row", "col"), split_axis=0, concat_axis=0, tiled=True)

    step = 640
    wire = pl.pallas_call(
        functools.partial(ffn_kernel, step),
        out_shape=jax.ShapeDtypeStruct((total * SUB, LANES), BF),
        in_specs=[vmem] * 4,
        out_specs=vmem,
        scratch_shapes=[pltpu.VMEM((step, width), BF)],
        compiler_params=limit,
        name="ffn",
    )(wire.reshape(total * SUB, LANES), w_gate[0], w_up[0], w_down[0])

    wire = wire.reshape(experts, slots * SUB, LANES)
    wire = lax.all_to_all(wire, ("row", "col"), split_axis=0, concat_axis=0, tiled=True)

    return pl.pallas_call(
        combine_kernel,
        out_shape=jax.ShapeDtypeStruct((rows, width), BF),
        in_specs=[smem, smem, vmem],
        out_specs=hbm,
        scratch_shapes=[
            pltpu.VMEM((2 * SUB, SUB, LANES), BF),
            pltpu.VMEM((rows, width), BF),
            pltpu.SemaphoreType.DMA((rows // (2 * SUB),)),
        ],
        compiler_params=limit,
        name="combine",
    )(pos, gate_probs.T, wire.reshape(total, SUB, LANES))


def solution(mesh):
    in_specs = (
        P(("row", "col"), None),
        P(("row", "col"), None),
        P(("row", "col"), None),
        P(("row", "col"), None, None),
        P(("row", "col"), None, None),
        P(("row", "col"), None, None),
    )
    out_specs = P(("row", "col"), None)
    return jax.shard_map(body, mesh=mesh, in_specs=in_specs, out_specs=out_specs, check_vma=False)
```

time: 175 us -> 172 us (0.983)
  no operation moved by 1% of the time
where the time goes in v3:
time: 172 us
  blocking collectives  149 us (87%)
  Pallas kernels  23.2 us (13%)
    all_to_all x2, blocking collectives, body(): lax.all_to_all(wire, ('row', 'col'), split_axis=0, concat_axis=0, tiled=T...  149 us
    pallas_call x1, Pallas kernels, body(): pl.pallas_call(functools.partial(ffn_kernel, step), out_shape=jax.ShapeDt...  15.5 us
    pallas_call x1, Pallas kernels, body(): pl.pallas_call(combine_kernel, out_shape=jax.ShapeDtypeStruct((rows, widt...  4.21 us
    pallas_call x1, Pallas kernels, body(): pl.pallas_call(functools.partial(dispatch_kernel, slots), out_shape=(jax....  3.47 us

profile of v3, /device:TPU:3, one launch (start us, length us, event | category | flops | bytes accessed | tf_op | source)
XLA Modules:
  0.0 172.0 jit_solution(14860183013839401603)
XLA Ops:
  0.0 3.5 %dispatch.1 = (bf16[1280,16,128]{2,1,0:T(8,128)(2,1)S(1)}, s32[8,128]{1,0:T(8,128)S(1)}) custom-call(s32[8,128]{1,0:T(8,128)} %bitcast.17, bf16[128,2048]{1,0:T(8,128)(2,1)} %tok_hbm.1), custom_call_target="tpu_custom_call" | custom-call | tf_op jit(solution)/shard_map/dispatch/pallas_call | solution.py:168
  3.5 0.0 copy-start
  3.5 0.0 copy-start.1
  3.5 0.0 copy-start.2
  3.5 76.2 %all_to_all.10 = bf16[128,160,128]{2,1,0:T(8,128)(2,1)S(1)} all-to-all(bf16[128,160,128]{2,1,0:T(8,128)(2,1)S(1)} %bitcast.12), channel_id=1, replica_groups=mesh['row'=8,'col'=16] {'row','col'}, dimensions={0} | all-to-all | bytes 10485760 | tf_op jit(solution)/shard_map/all_to_all | solution.py:188
  79.7 0.0 copy-done
  79.7 0.0 copy-done.1
  79.7 0.0 copy-done.2
  79.7 15.5 %ffn.1 = bf16[20480,128]{1,0:T(8,128)(2,1)S(1)} custom-call(bf16[20480,128]{1,0:T(8,128)(2,1)S(1)} %bitcast.10, bf16[2048,768]{1,0:T(8,128)(2,1)S(1)} %bitcast.13, bf16[2048,768]{1,0:T(8,128)(2,1)S(1)} %bitcast.14, bf16[768,2048]{1,0:T(8,128)(2,1)S(1)} %bitcast.15), custom_call_target="tpu_custom_call" | custom-call | tf_op jit(solution)/shard_map/ffn/pallas_call | solution.py:191
  95.3 0.0 copy-start.3
  95.3 72.5 %all_to_all.11 = bf16[128,160,128]{2,1,0:T(8,128)(2,1)S(1)} all-to-all(bf16[128,160,128]{2,1,0:T(8,128)(2,1)S(1)} %bitcast.11), channel_id=1, replica_groups=mesh['row'=8,'col'=16] {'row','col'}, dimensions={0} | all-to-all | bytes 10485760 | tf_op jit(solution)/shard_map/all_to_all | solution.py:202
  167.8 0.0 copy-done.3
  167.8 4.2 %combine.1 = bf16[128,2048]{1,0:T(8,128)(2,1)} custom-call(s32[8,128]{1,0:T(8,128)S(1)} %get-tuple-element.7.pos_ref, f32[8,128]{1,0:T(8,128)S(1)} %bitcast.16, bf16[1280,16,128]{2,1,0:T(8,128)(2,1)S(1)} %bitcast.9), custom_call_target="tpu_custom_call" | custom-call | tf_op jit(solution)/shard_map/combine/pallas_call | solution.py:204
Async XLA Ops:
  3.5 76.2 %copy-start = (bf16[1,2048,768]{2,1,0:T(8,128)(2,1)S(1)}, bf16[1,2048,768]{2,1,0:T(8,128)(2,1)}, u32[]{:S(2)}) copy-start(bf16[1,2048,768]{2,1,0:T(8,128)(2,1)} %param.9) | copy-start | bytes 9437188
  3.5 76.2 %copy-start.1 = (bf16[1,2048,768]{2,1,0:T(8,128)(2,1)S(1)}, bf16[1,2048,768]{2,1,0:T(8,128)(2,1)}, u32[]{:S(2)}) copy-start(bf16[1,2048,768]{2,1,0:T(8,128)(2,1)} %param.10) | copy-start | bytes 9437188
  3.5 76.2 %copy-start.2 = (bf16[1,768,2048]{2,1,0:T(8,128)(2,1)S(1)}, bf16[1,768,2048]{2,1,0:T(8,128)(2,1)}, u32[]{:S(2)}) copy-start(bf16[1,768,2048]{2,1,0:T(8,128)(2,1)} %param.11) | copy-start | bytes 9437188
  95.3 72.5 %copy-start.3 = (f32[128,8]{0,1:T(8,128)S(1)}, f32[128,8]{0,1:T(8,128)}, u32[]{:S(2)}) copy-start(f32[128,8]{0,1:T(8,128)} %param.8) | copy-start | bytes 12292

commit v4 on v3

--- a/solution.py
+++ b/solution.py
@@ -1,4 +1,5 @@
 import functools
+import math
 
 import jax
 import jax.numpy as jnp
@@ -43,7 +44,7 @@
     after = lax.broadcasted_iota(jnp.int32, (rows, rows), 1)
     earlier = (before < after).astype(F32).astype(BF)
     rank = jnp.dot(named.astype(BF), earlier, preferred_element_type=F32)
-    slot = expert.astype(F32) * slots + rank
+    slot = group_position(expert).astype(F32) * slots + rank
     for k in range(top):
         mine = jnp.where(ids[k : k + 1, :] == expert, slot, 0.0)
         pos_ref[k : k + 1, :] = jnp.sum(mine, axis=0, keepdims=True).astype(jnp.int32)
@@ -149,6 +150,20 @@
         put.wait()
 
 
+AXES = (("zh", 2), ("x", 4), ("zl", 2), ("y", 4), ("core", 2))
+ORDER = ("zh", "zl", "core", "x", "y")
+
+
+def group_position(expert):
+    digit, rest = {}, expert
+    for name, size in reversed(AXES):
+        digit[name], rest = rest % size, rest // size
+    place = jnp.zeros_like(expert)
+    for name in ORDER:
+        place = place * dict(AXES)[name] + digit[name]
+    return place
+
+
 def in_hbm(x):
     return pltpu.with_memory_space_constraint(x, pltpu.HBM)
 
@@ -157,7 +172,7 @@
     rows, top = expert_ids.shape
     width = tokens.shape[1]
     hidden = w_gate.shape[2]
-    experts = lax.axis_size("row") * lax.axis_size("col")
+    experts = math.prod(size for _, size in AXES)
     slots = 5 * rows * top // (4 * experts)
     total = experts * slots
     vmem = pl.BlockSpec(memory_space=pltpu.VMEM)
@@ -185,7 +200,7 @@
     )(in_hbm(expert_ids.T), in_hbm(tokens))
 
     wire = buffer.reshape(experts, slots * SUB, LANES)
-    wire = lax.all_to_all(wire, ("row", "col"), split_axis=0, concat_axis=0, tiled=True)
+    wire = lax.all_to_all(wire, ORDER, split_axis=0, concat_axis=0, tiled=True)
 
     step = 640
     wire = pl.pallas_call(
@@ -199,7 +214,7 @@
     )(wire.reshape(total * SUB, LANES), w_gate[0], w_up[0], w_down[0])
 
     wire = wire.reshape(experts, slots * SUB, LANES)
-    wire = lax.all_to_all(wire, ("row", "col"), split_axis=0, concat_axis=0, tiled=True)
+    wire = lax.all_to_all(wire, ORDER, split_axis=0, concat_axis=0, tiled=True)
 
     return pl.pallas_call(
         combine_kernel,
@@ -217,13 +232,12 @@
 
 
 def solution(mesh):
-    in_specs = (
-        P(("row", "col"), None),
-        P(("row", "col"), None),
-        P(("row", "col"), None),
-        P(("row", "col"), None, None),
-        P(("row", "col"), None, None),
-        P(("row", "col"), None, None),
+    names, sizes = zip(*AXES)
+    fine = jax.sharding.Mesh(mesh.devices.reshape(sizes), names)
+    return jax.shard_map(
+        body,
+        mesh=fine,
+        in_specs=(P(names, None),) * 3 + (P(names, None, None),) * 3,
+        out_specs=P(names, None),
+        check_vma=False,
     )
-    out_specs = P(("row", "col"), None)
-    return jax.shard_map(body, mesh=mesh, in_specs=in_specs, out_specs=out_specs, check_vma=False)

time: 172 us -> 167 us (0.971); the launches traced: 172 us -> 165 us
  blocking collectives: 149 us -> 141 us
    all_to_all x2, blocking collectives: 149 us -> 141 us  [body(): wire = lax.all_to_all(wire, ORDER, split_axis=0, concat_axis=0, tiled=True)]
where the time goes in v4:
time: 167 us; the launch traced here: 165 us
  blocking collectives  141 us (84%)
  Pallas kernels  23.2 us (14%)
    all_to_all x2, blocking collectives, body(): wire = lax.all_to_all(wire, ORDER, split_axis=0, concat_axis=0, tiled=True)  141 us
    pallas_call x1, Pallas kernels, body(): pl.pallas_call(functools.partial(ffn_kernel, step), out_shape=jax.ShapeDt...  15.5 us
    pallas_call x1, Pallas kernels, body(): pl.pallas_call(combine_kernel, out_shape=jax.ShapeDtypeStruct((rows, widt...  4.21 us
    pallas_call x1, Pallas kernels, body(): pl.pallas_call(functools.partial(dispatch_kernel, slots), out_shape=(jax....  3.53 us

profile of v4, /device:TPU:3, one launch (start us, length us, event | category | flops | bytes accessed | tf_op | source)
XLA Modules:
  0.0 164.5 jit_solution(4274379273815656185)
XLA Ops:
  0.0 3.5 %dispatch.1 = (bf16[1280,16,128]{2,1,0:T(8,128)(2,1)S(1)}, s32[8,128]{1,0:T(8,128)S(1)}) custom-call(s32[8,128]{1,0:T(8,128)} %bitcast.17, bf16[128,2048]{1,0:T(8,128)(2,1)} %tok_hbm.1), custom_call_target="tpu_custom_call" | custom-call | tf_op jit(solution)/shard_map/dispatch/pallas_call | solution.py:183
  3.5 0.0 copy-start
  3.5 0.0 copy-start.1
  3.6 0.0 copy-start.2
  3.6 73.1 %all_to_all.10 = bf16[128,160,128]{2,1,0:T(8,128)(2,1)S(1)} all-to-all(bf16[128,160,128]{2,1,0:T(8,128)(2,1)S(1)} %bitcast.12), channel_id=1, replica_groups=mesh['zh'=2,'x'=4,'zl'=2,'y'=4,'core'=2] {'zh','zl','core','x','y'}, dimensions={0} | all-to-all | bytes 10485760 | tf_op jit(solution)/shard_map/all_to_all | solution.py:203
  76.7 0.0 copy-done
  76.7 0.0 copy-done.1
  76.7 0.0 copy-done.2
  76.7 15.5 %ffn.1 = bf16[20480,128]{1,0:T(8,128)(2,1)S(1)} custom-call(bf16[20480,128]{1,0:T(8,128)(2,1)S(1)} %bitcast.10, bf16[2048,768]{1,0:T(8,128)(2,1)S(1)} %bitcast.13, bf16[2048,768]{1,0:T(8,128)(2,1)S(1)} %bitcast.14, bf16[768,2048]{1,0:T(8,128)(2,1)S(1)} %bitcast.15), custom_call_target="tpu_custom_call" | custom-call | tf_op jit(solution)/shard_map/ffn/pallas_call | solution.py:206
  92.2 0.0 copy-start.3
  92.2 68.1 %all_to_all.11 = bf16[128,160,128]{2,1,0:T(8,128)(2,1)S(1)} all-to-all(bf16[128,160,128]{2,1,0:T(8,128)(2,1)S(1)} %bitcast.11), channel_id=1, replica_groups=mesh['zh'=2,'x'=4,'zl'=2,'y'=4,'core'=2] {'zh','zl','core','x','y'}, dimensions={0} | all-to-all | bytes 10485760 | tf_op jit(solution)/shard_map/all_to_all | solution.py:217
  160.3 0.0 copy-done.3
  160.3 4.2 %combine.1 = bf16[128,2048]{1,0:T(8,128)(2,1)} custom-call(s32[8,128]{1,0:T(8,128)S(1)} %get-tuple-element.7.pos_ref, f32[8,128]{1,0:T(8,128)S(1)} %bitcast.16, bf16[1280,16,128]{2,1,0:T(8,128)(2,1)S(1)} %bitcast.9), custom_call_target="tpu_custom_call" | custom-call | tf_op jit(solution)/shard_map/combine/pallas_call | solution.py:219
Async XLA Ops:
  3.5 73.2 %copy-start = (bf16[1,2048,768]{2,1,0:T(8,128)(2,1)S(1)}, bf16[1,2048,768]{2,1,0:T(8,128)(2,1)}, u32[]{:S(2)}) copy-start(bf16[1,2048,768]{2,1,0:T(8,128)(2,1)} %param.9) | copy-start | bytes 9437188
  3.5 73.2 %copy-start.1 = (bf16[1,2048,768]{2,1,0:T(8,128)(2,1)S(1)}, bf16[1,2048,768]{2,1,0:T(8,128)(2,1)}, u32[]{:S(2)}) copy-start(bf16[1,2048,768]{2,1,0:T(8,128)(2,1)} %param.10) | copy-start | bytes 9437188
  3.6 73.2 %copy-start.2 = (bf16[1,768,2048]{2,1,0:T(8,128)(2,1)S(1)}, bf16[1,768,2048]{2,1,0:T(8,128)(2,1)}, u32[]{:S(2)}) copy-start(bf16[1,768,2048]{2,1,0:T(8,128)(2,1)} %param.11) | copy-start | bytes 9437188
  92.2 68.1 %copy-start.3 = (f32[128,8]{0,1:T(8,128)S(1)}, f32[128,8]{0,1:T(8,128)}, u32[]{:S(2)}) copy-start(f32[128,8]{0,1:T(8,128)} %param.8) | copy-start | bytes 12292

commit v5 on v4

v5 whole, which is shorter than its diff:
```python
import functools
import math

import jax
import jax.numpy as jnp
from jax import lax
from jax.experimental import pallas as pl
from jax.experimental.pallas import tpu as pltpu
from jax.sharding import PartitionSpec as P

BF = jnp.bfloat16
F32 = jnp.float32
LANES = 128
SUB = 16


def swap_matrix():
    i = lax.broadcasted_iota(jnp.int32, (SUB * SUB, SUB * SUB), 0)
    j = lax.broadcasted_iota(jnp.int32, (SUB * SUB, SUB * SUB), 1)
    return (j == (i % SUB) * SUB + i // SUB).astype(F32).astype(BF)


def dispatch_kernel(
    slots, ids_hbm, prob_hbm, tok_hbm, out_ref, mix_ref, ids_ref, prob_ref, pos_ref, tok_ref, tiles, pos_smem, sems
):
    top, rows = ids_ref.shape
    experts = out_ref.shape[0] // slots
    get_ids = pltpu.make_async_copy(ids_hbm, ids_ref, sems.at[0])
    get_tok = pltpu.make_async_copy(tok_hbm, tok_ref, sems.at[1])
    get_prob = pltpu.make_async_copy(prob_hbm, prob_ref, sems.at[3])
    get_ids.start()
    get_prob.start()
    get_tok.start()

    def clear(i, _):
        for j in range(4 * slots):
            out_ref[i * (4 * slots) + j] = jnp.zeros((SUB, LANES), BF)
        return 0

    lax.fori_loop(0, experts // 4, clear, 0)
    get_ids.wait()
    ids = group_position(ids_ref[...])
    expert = lax.broadcasted_iota(jnp.int32, (experts, rows), 0)
    named = jnp.zeros((experts, rows), F32)
    for k in range(top):
        named += (ids[k : k + 1, :] == expert).astype(F32)
    before = lax.broadcasted_iota(jnp.int32, (rows, rows), 0)
    after = lax.broadcasted_iota(jnp.int32, (rows, rows), 1)
    earlier = (before < after).astype(F32).astype(BF)
    rank = jnp.dot(named.astype(BF), earlier, preferred_element_type=F32)
    slot = expert.astype(F32) * slots + rank
    for k in range(top):
        mine = jnp.where(ids[k : k + 1, :] == expert, slot, 0.0)
        pos_ref[k : k + 1, :] = jnp.sum(mine, axis=0, keepdims=True).astype(jnp.int32)
    to_smem = pltpu.make_async_copy(pos_ref, pos_smem, sems.at[2])
    to_smem.start()
    get_prob.wait()
    weigh(slots, ids, prob_ref[...], named, rank, mix_ref)

    get_tok.wait()
    swap = swap_matrix()
    for b in range(rows // (2 * SUB)):
        halves = []
        for h in range(2):
            at = (2 * b + h) * SUB
            halves.append(
                jnp.concatenate(
                    [tok_ref[at : at + SUB, c * LANES : (c + 1) * LANES] for c in range(SUB)], axis=0
                )
            )
        moved = jnp.dot(swap, jnp.concatenate(halves, axis=1), preferred_element_type=F32).astype(BF)
        for h in range(2):
            at = (2 * b + h) * SUB
            tiles[at : at + SUB] = moved[:, h * LANES : (h + 1) * LANES].reshape(SUB, SUB, LANES)
    to_smem.wait()

    def place(i, _):
        for j in range(4):
            t = i * 4 + j
            tile = tiles[t]
            for k in range(top):
                out_ref[pos_smem[k, t]] = tile
        return 0

    lax.fori_loop(0, rows // 4, place, 0)


def pair_matrix(to_pairs):
    i = lax.broadcasted_iota(jnp.int32, (256, 256), 0)
    j = lax.broadcasted_iota(jnp.int32, (256, 256), 1)
    if to_pairs:
        source = (i // 2 % SUB) * 16 + (i // 32) * 2 + i % 2
    else:
        source = (i // 2 % 8) * 32 + (i // 16) * 2 + i % 2
    return (j == source).astype(F32).astype(BF)


def ffn_kernel(slots, x_ref, wg_ref, wu_ref, wd_ref, out_ref, rows_ref, tail_ref):
    swap = swap_matrix()
    sources = out_ref.shape[0]
    chunk = slots * SUB
    main = 8 * sources
    groups = []
    for g in range(sources // 2):
        groups.append([(2 * g + h) * chunk for h in range(2)])
    for g in range(sources // 8):
        groups.append([(8 * g + h) * chunk + 8 * SUB for h in range(8)])
    for b in range(len(groups) // 2):
        halves = []
        for h in range(2):
            starts = groups[2 * b + h]
            size = 256 // len(starts)
            halves.append(jnp.concatenate([x_ref[at : at + size, :] for at in starts], axis=0))
        moved = jnp.dot(swap, jnp.concatenate(halves, axis=1), preferred_element_type=F32).astype(BF)
        for h in range(2):
            for c in range(SUB):
                rows_ref[(2 * b + h) * SUB : (2 * b + h + 1) * SUB, c * LANES : (c + 1) * LANES] = moved[
                    c * SUB : (c + 1) * SUB, h * LANES : (h + 1) * LANES
                ]
    x = rows_ref[...]
    gate = jnp.dot(x, wg_ref[...], preferred_element_type=F32)
    up = jnp.dot(x, wu_ref[...], preferred_element_type=F32)
    hidden = (gate / (1.0 + jnp.exp(-gate)) * up).astype(BF)
    for n in range(SUB // 2):
        cols = slice(n * 256, (n + 1) * 256)
        result = jnp.dot(hidden, wd_ref[:, cols], preferred_element_type=F32).astype(BF)
        for h in range(2):
            half = result[:, h * LANES : (h + 1) * LANES]
            out_ref[:, 2 * n + h] = half[:main].reshape(sources, 8, LANES)
        tail_ref[:, cols] = result[main:]
    pairs = pair_matrix(True)
    for b in range(sources // 16):
        halves = []
        for h in range(2):
            at = (2 * b + h) * SUB
            halves.append(
                jnp.concatenate(
                    [tail_ref[at : at + SUB, c * LANES : (c + 1) * LANES] for c in range(SUB)], axis=0
                )
            )
        moved = jnp.dot(pairs, jnp.concatenate(halves, axis=1), preferred_element_type=F32).astype(BF)
        for h in range(2):
            at = (2 * b + h) * 8
            out_ref[at : at + 8, SUB : 2 * slots] = moved[:, h * LANES : (h + 1) * LANES].reshape(
                8, 2 * slots - SUB, 8, LANES
            )


def weigh(slots, place, prob, named, rank, out_ref):
    top, rows = place.shape
    total = out_ref.shape[1]
    experts = total // slots
    expert = lax.broadcasted_iota(jnp.int32, (experts, rows), 0)
    weight = jnp.zeros((experts, rows), F32)
    for k in range(top):
        weight += jnp.where(place[k : k + 1, :] == expert, prob[k : k + 1, :], 0.0)
    rank = jnp.where(named > 0.0, rank, -1.0).T.astype(BF)
    weight = weight.T
    high = weight.astype(BF)
    low = (weight - high.astype(F32)).astype(BF)
    col = lax.broadcasted_iota(jnp.int32, (experts, total), 1)
    main = 8 * experts
    owner = jnp.where(col < main, col // 8, (col - main) // (slots - 8))
    spread = (owner == lax.broadcasted_iota(jnp.int32, (experts, total), 0)).astype(F32).astype(BF)
    col = lax.broadcasted_iota(jnp.int32, (rows, total), 1)
    slot = jnp.where(col < main, col % 8, 8 + (col - main) % (slots - 8)).astype(F32)
    mine = jnp.dot(rank, spread, preferred_element_type=F32) == slot
    for i, part in enumerate((high, low)):
        wide = jnp.dot(part, spread, preferred_element_type=F32)
        out_ref[i * rows : (i + 1) * rows, :] = jnp.where(mine, wide, 0.0).astype(BF)


def combine_kernel(slots, mix_ref, x_ref, out_hbm, tail_ref, out_ref, sems):
    experts = x_ref.shape[0]
    rows = out_ref.shape[0]
    main = 8 * experts
    pairs = pair_matrix(False)
    for b in range(experts // 16):
        halves = []
        for h in range(2):
            at = (2 * b + h) * 8
            halves.append(x_ref[at : at + 8, SUB : 2 * slots].reshape(256, LANES))
        moved = jnp.dot(pairs, jnp.concatenate(halves, axis=1), preferred_element_type=F32).astype(BF)
        for h in range(2):
            at = (2 * b + h) * SUB
            for c in range(SUB):
                tail_ref[at : at + SUB, c * LANES : (c + 1) * LANES] = moved[
                    c * SUB : (c + 1) * SUB, h * LANES : (h + 1) * LANES
                ]
    copies = []
    for n in range(SUB // 2):
        cols = slice(n * 256, (n + 1) * 256)
        block = jnp.concatenate([x_ref[:, 2 * n + h].reshape(main, LANES) for h in range(2)], axis=1)
        mixed = jnp.dot(mix_ref[:, :main], block, preferred_element_type=F32)
        mixed += jnp.dot(mix_ref[:, main:], tail_ref[:, cols], preferred_element_type=F32)
        out_ref[:, cols] = (mixed[:rows] + mixed[rows:]).astype(BF)
        if n % 4 == 3:
            part = pl.ds((n // 4) * 1024, 1024)
            put = pltpu.make_async_copy(out_ref.at[:, part], out_hbm.at[:, part], sems.at[n // 4])
            put.start()
            copies.append(put)
    for put in copies:
        put.wait()


AXES = (("zh", 2), ("x", 4), ("zl", 2), ("y", 4), ("core", 2))
ORDER = ("zh", "zl", "core", "x", "y")


def group_position(expert):
    digit, rest = {}, expert
    for name, size in reversed(AXES):
        digit[name], rest = rest % size, rest // size
    place = jnp.zeros_like(expert)
    for name in ORDER:
        place = place * dict(AXES)[name] + digit[name]
    return place


def in_hbm(x):
    return pltpu.with_memory_space_constraint(x, pltpu.HBM)


def body(tokens, expert_ids, gate_probs, w_gate, w_up, w_down):
    rows, top = expert_ids.shape
    width = tokens.shape[1]
    hidden = w_gate.shape[2]
    experts = math.prod(size for _, size in AXES)
    slots = 5 * rows * top // (4 * experts)
    total = experts * slots
    vmem = pl.BlockSpec(memory_space=pltpu.VMEM)
    hbm = pl.BlockSpec(memory_space=pltpu.HBM)
    limit = pltpu.CompilerParams(vmem_limit_bytes=32 * 1024 * 1024)

    buffer, mix = pl.pallas_call(
        functools.partial(dispatch_kernel, slots),
        out_shape=(
            jax.ShapeDtypeStruct((total, SUB, LANES), BF),
            jax.ShapeDtypeStruct((2 * rows, total), BF),
        ),
        in_specs=[hbm, hbm, hbm],
        out_specs=(vmem, vmem),
        scratch_shapes=[
            pltpu.VMEM((top, rows), jnp.int32),
            pltpu.VMEM((top, rows), F32),
            pltpu.VMEM((top, rows), jnp.int32),
            pltpu.VMEM((rows, width), BF),
            pltpu.VMEM((rows, SUB, LANES), BF),
            pltpu.SMEM((top, rows), jnp.int32),
            pltpu.SemaphoreType.DMA((4,)),
        ],
        compiler_params=limit,
        name="dispatch",
    )(in_hbm(expert_ids.T), in_hbm(gate_probs.T), in_hbm(tokens))

    wire = buffer.reshape(experts, slots * SUB, LANES)
    wire = lax.all_to_all(wire, ORDER, split_axis=0, concat_axis=0, tiled=True)

    wire = pl.pallas_call(
        functools.partial(ffn_kernel, slots),
        out_shape=jax.ShapeDtypeStruct((experts, 2 * slots, 8, LANES), BF),
        in_specs=[vmem] * 4,
        out_specs=vmem,
        scratch_shapes=[pltpu.VMEM((total, width), BF), pltpu.VMEM((total - 8 * experts, width), BF)],
        compiler_params=limit,
        name="ffn",
    )(wire.reshape(total * SUB, LANES), w_gate[0], w_up[0], w_down[0])

    wire = wire.reshape(experts, slots * SUB, LANES)
    wire = lax.all_to_all(wire, ORDER, split_axis=0, concat_axis=0, tiled=True)

    return pl.pallas_call(
        functools.partial(combine_kernel, slots),
        out_shape=jax.ShapeDtypeStruct((rows, width), BF),
        in_specs=[vmem, vmem],
        out_specs=hbm,
        scratch_shapes=[
            pltpu.VMEM((total - 8 * experts, width), BF),
            pltpu.VMEM((rows, width), BF),
            pltpu.SemaphoreType.DMA((2,)),
        ],
        compiler_params=limit,
        name="combine",
    )(mix, wire.reshape(experts, 2 * slots, 8, LANES))


def solution(mesh):
    names, sizes = zip(*AXES)
    fine = jax.sharding.Mesh(mesh.devices.reshape(sizes), names)
    return jax.shard_map(
        body,
        mesh=fine,
        in_specs=(P(names, None),) * 3 + (P(names, None, None),) * 3,
        out_specs=P(names, None),
        check_vma=False,
    )
```

time: 167 us -> 164 us (0.982)
  Pallas kernels: 23.2 us -> 20.6 us
    pallas_call x2, Pallas kernels: 19.7 us -> 16.9 us  [the longest x1 14.3 us: body(): pl.pallas_call(functools.partial(ffn_kernel, slots), out_shape=jax.ShapeD...]
where the time goes in v5:
time: 164 us; the launch traced here: 162 us
  blocking collectives  141 us (86%)
  Pallas kernels  20.6 us (13%)
    all_to_all x2, blocking collectives, body(): wire = lax.all_to_all(wire, ORDER, split_axis=0, concat_axis=0, tiled=True)  141 us
    pallas_call x1, Pallas kernels, body(): pl.pallas_call(functools.partial(ffn_kernel, slots), out_shape=jax.ShapeD...  14.3 us
    pallas_call x1, Pallas kernels, body(): pl.pallas_call(functools.partial(dispatch_kernel, slots), out_shape=(jax....  3.73 us

profile of v5, /device:TPU:3, one launch (start us, length us, event | category | flops | bytes accessed | tf_op | source)
XLA Modules:
  0.0 161.9 jit_solution(1102562778897701227)
XLA Ops:
  0.0 3.7 %dispatch.1 = (bf16[1280,16,128]{2,1,0:T(8,128)(2,1)S(1)}, bf16[256,1280]{1,0:T(8,128)(2,1)S(1)}) custom-call(s32[8,128]{1,0:T(8,128)} %bitcast.16, f32[8,128]{1,0:T(8,128)} %bitcast.17, bf16[128,2048]{1,0:T(8,128)(2,1)} %tok_hbm.1), custom_call_target="tpu_custom_call" | custom-call | tf_op jit(solution)/shard_map/dispatch/pallas_call | solution.py:235
  3.7 0.0 copy-start
  3.8 0.0 copy-start.1
  3.8 0.0 copy-start.2
  3.8 73.1 %all_to_all.10 = bf16[128,160,128]{2,1,0:T(8,128)(2,1)S(1)} all-to-all(bf16[128,160,128]{2,1,0:T(8,128)(2,1)S(1)} %bitcast.12), channel_id=1, replica_groups=mesh['zh'=2,'x'=4,'zl'=2,'y'=4,'core'=2] {'zh','zl','core','x','y'}, dimensions={0} | all-to-all | bytes 10485760 | tf_op jit(solution)/shard_map/all_to_all | solution.py:257
  76.9 0.0 copy-done
  76.9 0.0 copy-done.1
  76.9 0.0 copy-done.2
  76.9 14.3 %ffn.1 = bf16[128,20,8,128]{3,2,1,0:T(8,128)(2,1)S(1)} custom-call(bf16[20480,128]{1,0:T(8,128)(2,1)S(1)} %bitcast.10, bf16[2048,768]{1,0:T(8,128)(2,1)S(1)} %bitcast.13, bf16[2048,768]{1,0:T(8,128)(2,1)S(1)} %bitcast.14, bf16[768,2048]{1,0:T(8,128)(2,1)S(1)} %bitcast.15), custom_call_target="tpu_custom_call" | custom-call | tf_op jit(solution)/shard_map/ffn/pallas_call | solution.py:259
  91.2 68.1 %all_to_all.11 = bf16[128,160,128]{2,1,0:T(8,128)(2,1)S(1)} all-to-all(bf16[128,160,128]{2,1,0:T(8,128)(2,1)S(1)} %bitcast.11), channel_id=1, replica_groups=mesh['zh'=2,'x'=4,'zl'=2,'y'=4,'core'=2] {'zh','zl','core','x','y'}, dimensions={0} | all-to-all | bytes 10485760 | tf_op jit(solution)/shard_map/all_to_all | solution.py:270
  159.3 2.6 %combine.1 = bf16[128,2048]{1,0:T(8,128)(2,1)} custom-call(bf16[256,1280]{1,0:T(8,128)(2,1)S(1)} %get-tuple-element.7.mix_ref, bf16[128,20,8,128]{3,2,1,0:T(8,128)(2,1)S(1)} %bitcast.9), custom_call_target="tpu_custom_call" | custom-call | tf_op jit(solution)/shard_map/combine/pallas_call | solution.py:272
Async XLA Ops:
  3.7 73.2 %copy-start = (bf16[1,2048,768]{2,1,0:T(8,128)(2,1)S(1)}, bf16[1,2048,768]{2,1,0:T(8,128)(2,1)}, u32[]{:S(2)}) copy-start(bf16[1,2048,768]{2,1,0:T(8,128)(2,1)} %param.9) | copy-start | bytes 9437188
  3.8 73.2 %copy-start.1 = (bf16[1,2048,768]{2,1,0:T(8,128)(2,1)S(1)}, bf16[1,2048,768]{2,1,0:T(8,128)(2,1)}, u32[]{:S(2)}) copy-start(bf16[1,2048,768]{2,1,0:T(8,128)(2,1)} %param.10) | copy-start | bytes 9437188
  3.8 73.2 %copy-start.2 = (bf16[1,768,2048]{2,1,0:T(8,128)(2,1)S(1)}, bf16[1,768,2048]{2,1,0:T(8,128)(2,1)}, u32[]{:S(2)}) copy-start(bf16[1,768,2048]{2,1,0:T(8,128)(2,1)} %param.11) | copy-start | bytes 9437188

commit v6 on v0

v6 whole, which is shorter than its diff:
```python
import functools
import math

import jax
import jax.numpy as jnp
from jax import lax
from jax.experimental import pallas as pl
from jax.experimental.pallas import tpu as pltpu
from jax.sharding import PartitionSpec as P

BF = jnp.bfloat16
F32 = jnp.float32
LANES = 128
SUB = 16


def pair_matrix(to_pairs):
    i = lax.broadcasted_iota(jnp.int32, (256, 256), 0)
    j = lax.broadcasted_iota(jnp.int32, (256, 256), 1)
    if to_pairs:
        source = (i // 2 % SUB) * 16 + (i // 32) * 2 + i % 2
    else:
        source = (i // 2 % 8) * 32 + (i // 16) * 2 + i % 2
    return (j == source).astype(F32).astype(BF)


def store_pairs(tail_ref, chunks):
    peers, tiles = chunks.shape[:2]
    pairs = pair_matrix(True)
    for b in range(peers // 16):
        halves = []
        for h in range(2):
            at = (2 * b + h) * SUB
            halves.append(
                jnp.concatenate(
                    [tail_ref[at : at + SUB, c * LANES : (c + 1) * LANES] for c in range(SUB)], axis=0
                )
            )
        moved = jnp.dot(pairs, jnp.concatenate(halves, axis=1), preferred_element_type=F32).astype(BF)
        for h in range(2):
            at = (2 * b + h) * 8
            chunks[at : at + 8, SUB:tiles] = moved[:, h * LANES : (h + 1) * LANES].reshape(8, tiles - SUB, 8, LANES)


def load_pairs(chunks, tail_ref):
    peers, tiles = chunks.shape[:2]
    pairs = pair_matrix(False)
    for b in range(peers // 16):
        halves = []
        for h in range(2):
            at = (2 * b + h) * 8
            halves.append(chunks[at : at + 8, SUB:tiles].reshape(256, LANES))
        moved = jnp.dot(pairs, jnp.concatenate(halves, axis=1), preferred_element_type=F32).astype(BF)
        for h in range(2):
            at = (2 * b + h) * SUB
            for c in range(SUB):
                tail_ref[at : at + SUB, c * LANES : (c + 1) * LANES] = moved[
                    c * SUB : (c + 1) * SUB, h * LANES : (h + 1) * LANES
                ]


def store_columns(result, n, chunks, tail_ref):
    peers = chunks.shape[0]
    main = 8 * peers
    for h in range(2):
        half = result[:, h * LANES : (h + 1) * LANES]
        chunks[:, 2 * n + h] = half[:main].reshape(peers, 8, LANES)
    tail_ref[:, n * 256 : (n + 1) * 256] = result[main:]


def columns_of(chunks, n):
    main = 8 * chunks.shape[0]
    return jnp.concatenate([chunks[:, 2 * n + h].reshape(main, LANES) for h in range(2)], axis=1)


def owner_and_slot(index, slots, experts):
    main = 8 * experts
    owner = jnp.where(index < main, index // 8, (index - main) // (slots - 8))
    slot = jnp.where(index < main, index % 8, 8 + (index - main) % (slots - 8))
    return owner, slot


def dispatch_kernel(slots, ids_hbm, prob_hbm, tok_hbm, out_ref, mix_ref, ids_ref, prob_ref, tok_ref, tail_ref, sems):
    top, rows = ids_ref.shape
    experts = out_ref.shape[0]
    total = experts * slots
    get_ids = pltpu.make_async_copy(ids_hbm, ids_ref, sems.at[0])
    get_prob = pltpu.make_async_copy(prob_hbm, prob_ref, sems.at[1])
    get_tok = pltpu.make_async_copy(tok_hbm, tok_ref, sems.at[2])
    get_ids.start()
    get_prob.start()
    get_tok.start()

    before = lax.broadcasted_iota(jnp.int32, (rows, rows), 0)
    after = lax.broadcasted_iota(jnp.int32, (rows, rows), 1)
    earlier = (before < after).astype(F32).astype(BF)
    owner, slot = owner_and_slot(lax.broadcasted_iota(jnp.int32, (total, experts), 0), slots, experts)
    from_expert = (owner == lax.broadcasted_iota(jnp.int32, (total, experts), 1)).astype(F32).astype(BF)
    get_ids.wait()
    get_prob.wait()
    place = group_position(ids_ref[...])
    prob = prob_ref[...]
    expert = lax.broadcasted_iota(jnp.int32, (experts, rows), 0)
    named = jnp.zeros((experts, rows), F32)
    weight = jnp.zeros((experts, rows), F32)
    for k in range(top):
        mine = place[k : k + 1, :] == expert
        named += mine.astype(F32)
        weight += jnp.where(mine, prob[k : k + 1, :], 0.0)
    rank = jnp.dot(named.astype(BF), earlier, preferred_element_type=F32)
    rank = jnp.where(named > 0.0, rank, -1.0)
    ranks = jnp.dot(from_expert, rank.astype(BF), preferred_element_type=F32)
    picked = (ranks == slot.astype(F32)).astype(F32).astype(BF)
    get_tok.wait()
    for n in range(SUB // 2):
        cols = slice(n * 256, (n + 1) * 256)
        store_columns(jnp.dot(picked, tok_ref[:, cols], preferred_element_type=F32).astype(BF), n, out_ref, tail_ref)
    store_pairs(tail_ref, out_ref)

    rank = rank.T.astype(BF)
    weight = weight.T
    high = weight.astype(BF)
    low = (weight - high.astype(F32)).astype(BF)
    owner, _ = owner_and_slot(lax.broadcasted_iota(jnp.int32, (experts, total), 1), slots, experts)
    _, slot = owner_and_slot(lax.broadcasted_iota(jnp.int32, (rows, total), 1), slots, experts)
    to_slot = (owner == lax.broadcasted_iota(jnp.int32, (experts, total), 0)).astype(F32).astype(BF)
    mine = jnp.dot(rank, to_slot, preferred_element_type=F32) == slot.astype(F32)
    for i, part in enumerate((high, low)):
        wide = jnp.dot(part, to_slot, preferred_element_type=F32)
        mix_ref[i * rows : (i + 1) * rows, :] = jnp.where(mine, wide, 0.0).astype(BF)


def ffn_kernel(x_ref, wg_ref, wu_ref, wd_ref, out_ref, rows_ref, tail_ref):
    main = 8 * x_ref.shape[0]
    load_pairs(x_ref, rows_ref.at[pl.ds(main, rows_ref.shape[0] - main), :])
    for n in range(SUB // 2):
        rows_ref[:main, n * 256 : (n + 1) * 256] = columns_of(x_ref, n)
    x = rows_ref[...]
    gate = jnp.dot(x, wg_ref[...], preferred_element_type=F32)
    up = jnp.dot(x, wu_ref[...], preferred_element_type=F32)
    hidden = (gate / (1.0 + jnp.exp(-gate)) * up).astype(BF)
    for n in range(SUB // 2):
        cols = slice(n * 256, (n + 1) * 256)
        store_columns(jnp.dot(hidden, wd_ref[:, cols], preferred_element_type=F32).astype(BF), n, out_ref, tail_ref)
    store_pairs(tail_ref, out_ref)


def combine_kernel(mix_ref, x_ref, out_hbm, tail_ref, out_ref, sems):
    rows = out_ref.shape[0]
    main = 8 * x_ref.shape[0]
    load_pairs(x_ref, tail_ref)
    copies = []
    for n in range(SUB // 2):
        cols = slice(n * 256, (n + 1) * 256)
        mixed = jnp.dot(mix_ref[:, :main], columns_of(x_ref, n), preferred_element_type=F32)
        mixed += jnp.dot(mix_ref[:, main:], tail_ref[:, cols], preferred_element_type=F32)
        out_ref[:, cols] = (mixed[:rows] + mixed[rows:]).astype(BF)
        if n % 4 == 3:
            part = pl.ds((n // 4) * 1024, 1024)
            put = pltpu.make_async_copy(out_ref.at[:, part], out_hbm.at[:, part], sems.at[n // 4])
            put.start()
            copies.append(put)
    for put in copies:
        put.wait()


AXES = (("zh", 2), ("x", 4), ("zl", 2), ("y", 4), ("core", 2))
ORDER = ("zh", "zl", "core", "x", "y")


def group_position(expert):
    digit, rest = {}, expert
    for name, size in reversed(AXES):
        digit[name], rest = rest % size, rest // size
    place = jnp.zeros_like(expert)
    for name in ORDER:
        place = place * dict(AXES)[name] + digit[name]
    return place


def in_hbm(x):
    return pltpu.with_memory_space_constraint(x, pltpu.HBM)


def body(tokens, expert_ids, gate_probs, w_gate, w_up, w_down):
    rows, top = expert_ids.shape
    width = tokens.shape[1]
    experts = math.prod(size for _, size in AXES)
    slots = 5 * rows * top // (4 * experts)
    total = experts * slots
    vmem = pl.BlockSpec(memory_space=pltpu.VMEM)
    hbm = pl.BlockSpec(memory_space=pltpu.HBM)
    limit = pltpu.CompilerParams(vmem_limit_bytes=32 * 1024 * 1024)
    chunks = jax.ShapeDtypeStruct((experts, 2 * slots, 8, LANES), BF)
    tail = pltpu.VMEM((total - 8 * experts, width), BF)

    def exchange(x):
        wire = x.reshape(experts, slots * SUB, LANES)
        wire = lax.all_to_all(wire, ORDER, split_axis=0, concat_axis=0, tiled=True)
        return wire.reshape(chunks.shape)

    sent, mix = pl.pallas_call(
        functools.partial(dispatch_kernel, slots),
        out_shape=(chunks, jax.ShapeDtypeStruct((2 * rows, total), BF)),
        in_specs=[hbm, hbm, hbm],
        out_specs=(vmem, vmem),
        scratch_shapes=[
            pltpu.VMEM((top, rows), jnp.int32),
            pltpu.VMEM((top, rows), F32),
            pltpu.VMEM((rows, width), BF),
            tail,
            pltpu.SemaphoreType.DMA((3,)),
        ],
        compiler_params=limit,
        name="dispatch",
    )(in_hbm(expert_ids.T), in_hbm(gate_probs.T), in_hbm(tokens))

    made = pl.pallas_call(
        ffn_kernel,
        out_shape=chunks,
        in_specs=[vmem] * 4,
        out_specs=vmem,
        scratch_shapes=[pltpu.VMEM((total, width), BF), tail],
        compiler_params=limit,
        name="ffn",
    )(exchange(sent), w_gate[0], w_up[0], w_down[0])

    return pl.pallas_call(
        combine_kernel,
        out_shape=jax.ShapeDtypeStruct((rows, width), BF),
        in_specs=[vmem, vmem],
        out_specs=hbm,
        scratch_shapes=[tail, pltpu.VMEM((rows, width), BF), pltpu.SemaphoreType.DMA((2,))],
        compiler_params=limit,
        name="combine",
    )(mix, exchange(made))


def solution(mesh):
    names, sizes = zip(*AXES)
    fine = jax.sharding.Mesh(mesh.devices.reshape(sizes), names)
    return jax.shard_map(
        body,
        mesh=fine,
        in_specs=(P(names, None),) * 3 + (P(names, None, None),) * 3,
        out_specs=P(names, None),
        check_vma=False,
    )
```

time: 330 us -> 163 us (0.49); the launches traced: 324 us -> 161 us
  waiting for transfers between devices: 105 us -> 0 us
  local copies, waits for them, and re-layouts: 64.3 us -> 0.02 us
  blocking collectives: 114 us -> 141 us
  Pallas kernels: 0 us -> 19.3 us
  matrix products: 18.1 us -> 0 us
  starting transfers between devices: 11.1 us -> 0 us
  other arithmetic: 10.7 us -> 0 us
    all_to_all x1 -> x0, waiting for transfers between devices: 105 us -> none  [body(): lax.all_to_all(produced, ('row', 'col'), split_axis=0, concat_axis=0, til...]
    all_to_all x1 -> x2, blocking collectives: 114 us -> 141 us  [exchange(): wire = lax.all_to_all(wire, ORDER, split_axis=0, concat_axis=0, tiled=True)]
    reshape x2 -> x0, local copies, waits for them, and re-layouts: 19.4 us -> none  [the longest x1 9.84 us: body(): returned = returned.reshape(expert_count * slot_count, width)]
    another operation x4 -> x0, local copies, waits for them, and re-layouts: 19.4 us -> none  [the longest x1 9.85 us: apply_experts(): rows = received[:, 0].reshape(-1, width)]
    pallas_call x0 -> x3, Pallas kernels: none -> 19.3 us  [the longest x1 13.2 us: body(): pl.pallas_call(ffn_kernel, out_shape=chunks, in_specs=[vmem] * 4, out_spe...]
    dot_general x3 -> x0, matrix products: 18.1 us -> none  [the longest x1 7.24 us: apply_experts(): gate = jnp.dot(rows, w_gate[0], preferred_element_type=jnp.float32)]
    gather x1 -> x0, local copies, waits for them, and re-layouts: 12.1 us -> none  [body(): returned[target].reshape(tok_rows, choices_per, width).astype(jnp.float32)]
    all_to_all x1 -> x0, starting transfers between devices: 11.1 us -> none  [body(): lax.all_to_all(produced, ('row', 'col'), split_axis=0, concat_axis=0, til...]
  transfers between devices with their start and end apart: 1 -> 0, of which waited for: 1 -> 0; matrix products, arithmetic and copies ran while one was open for 0% -> 0% of each run, Pallas kernels for 0% -> 0%
where the time goes in v6:
time: 163 us; the launch traced here: 161 us
  blocking collectives  141 us (87%)
  Pallas kernels  19.3 us (12%)
    all_to_all x2, blocking collectives, exchange(): wire = lax.all_to_all(wire, ORDER, split_axis=0, concat_axis=0, tiled=True)  141 us
    pallas_call x1, Pallas kernels, body(): pl.pallas_call(ffn_kernel, out_shape=chunks, in_specs=[vmem] * 4, out_spe...  13.2 us
    pallas_call x1, Pallas kernels, body(): pl.pallas_call(functools.partial(dispatch_kernel, slots), out_shape=(chun...  3.5 us

profile of v6, /device:TPU:3, one launch (start us, length us, event | category | flops | bytes accessed | tf_op | source)
XLA Modules:
  0.0 160.7 jit_solution(6878536020979747319)
XLA Ops:
  0.0 3.5 %dispatch.1 = (bf16[128,20,8,128]{3,2,1,0:T(8,128)(2,1)S(1)}, bf16[256,1280]{1,0:T(8,128)(2,1)S(1)}) custom-call(s32[8,128]{1,0:T(8,128)} %bitcast.16, f32[8,128]{1,0:T(8,128)} %bitcast.17, bf16[128,2048]{1,0:T(8,128)(2,1)} %tok_hbm.1), custom_call_target="tpu_custom_call" | custom-call | tf_op jit(solution)/shard_map/dispatch/pallas_call | solution.py:202
  3.5 0.0 copy-start
  3.5 0.0 copy-start.1
  3.5 0.0 copy-start.2
  3.5 73.1 %all_to_all.10 = bf16[128,160,128]{2,1,0:T(8,128)(2,1)S(1)} all-to-all(bf16[128,160,128]{2,1,0:T(8,128)(2,1)S(1)} %bitcast.12), channel_id=1, replica_groups=mesh['zh'=2,'x'=4,'zl'=2,'y'=4,'core'=2] {'zh','zl','core','x','y'}, dimensions={0} | all-to-all | bytes 10485760 | tf_op jit(solution)/shard_map/all_to_all | solution.py:199
  76.7 0.0 copy-done
  76.7 0.0 copy-done.1
  76.7 0.0 copy-done.2
  76.7 13.2 %ffn.1 = bf16[128,20,8,128]{3,2,1,0:T(8,128)(2,1)S(1)} custom-call(bf16[128,20,8,128]{3,2,1,0:T(8,128)(2,1)S(1)} %bitcast.10, bf16[2048,768]{1,0:T(8,128)(2,1)S(1)} %bitcast.13, bf16[2048,768]{1,0:T(8,128)(2,1)S(1)} %bitcast.14, bf16[768,2048]{1,0:T(8,128)(2,1)S(1)} %bitcast.15), custom_call_target="tpu_custom_call" | custom-call | tf_op jit(solution)/shard_map/ffn/pallas_call | solution.py:218
  89.9 68.1 %all_to_all.11 = bf16[128,160,128]{2,1,0:T(8,128)(2,1)S(1)} all-to-all(bf16[128,160,128]{2,1,0:T(8,128)(2,1)S(1)} %bitcast.11), channel_id=1, replica_groups=mesh['zh'=2,'x'=4,'zl'=2,'y'=4,'core'=2] {'zh','zl','core','x','y'}, dimensions={0} | all-to-all | bytes 10485760 | tf_op jit(solution)/shard_map/all_to_all | solution.py:199
  158.0 2.6 %combine.1 = bf16[128,2048]{1,0:T(8,128)(2,1)} custom-call(bf16[256,1280]{1,0:T(8,128)(2,1)S(1)} %get-tuple-element.7.mix_ref, bf16[128,20,8,128]{3,2,1,0:T(8,128)(2,1)S(1)} %bitcast.9), custom_call_target="tpu_custom_call" | custom-call | tf_op jit(solution)/shard_map/combine/pallas_call | solution.py:228
Async XLA Ops:
  3.5 73.2 %copy-start = (bf16[1,2048,768]{2,1,0:T(8,128)(2,1)S(1)}, bf16[1,2048,768]{2,1,0:T(8,128)(2,1)}, u32[]{:S(2)}) copy-start(bf16[1,2048,768]{2,1,0:T(8,128)(2,1)} %param.9) | copy-start | bytes 9437188
  3.5 73.2 %copy-start.1 = (bf16[1,2048,768]{2,1,0:T(8,128)(2,1)S(1)}, bf16[1,2048,768]{2,1,0:T(8,128)(2,1)}, u32[]{:S(2)}) copy-start(bf16[1,2048,768]{2,1,0:T(8,128)(2,1)} %param.10) | copy-start | bytes 9437188
  3.5 73.2 %copy-start.2 = (bf16[1,768,2048]{2,1,0:T(8,128)(2,1)S(1)}, bf16[1,768,2048]{2,1,0:T(8,128)(2,1)}, u32[]{:S(2)}) copy-start(bf16[1,768,2048]{2,1,0:T(8,128)(2,1)} %param.11) | copy-start | bytes 9437188

commit v7 on v6

--- a/solution.py
+++ b/solution.py
@@ -136,9 +136,13 @@
     for n in range(SUB // 2):
         rows_ref[:main, n * 256 : (n + 1) * 256] = columns_of(x_ref, n)
     x = rows_ref[...]
-    gate = jnp.dot(x, wg_ref[...], preferred_element_type=F32)
-    up = jnp.dot(x, wu_ref[...], preferred_element_type=F32)
-    hidden = (gate / (1.0 + jnp.exp(-gate)) * up).astype(BF)
+    parts = []
+    for j in range(wg_ref.shape[1] // 256):
+        cols = slice(j * 256, (j + 1) * 256)
+        gate = jnp.dot(x, wg_ref[:, cols], preferred_element_type=F32)
+        up = jnp.dot(x, wu_ref[:, cols], preferred_element_type=F32)
+        parts.append((gate / (1.0 + jnp.exp(-gate)) * up).astype(BF))
+    hidden = jnp.concatenate(parts, axis=1)
     for n in range(SUB // 2):
         cols = slice(n * 256, (n + 1) * 256)
         store_columns(jnp.dot(hidden, wd_ref[:, cols], preferred_element_type=F32).astype(BF), n, out_ref, tail_ref)
@@ -165,7 +169,7 @@
 
 
 AXES = (("zh", 2), ("x", 4), ("zl", 2), ("y", 4), ("core", 2))
-ORDER = ("zh", "zl", "core", "x", "y")
+ORDER = ("zl", "y", "core", "x", "zh")
 
 
 def group_position(expert):

time: 163 us -> 162 us (level)
  no operation moved by 1% of the time
where the time goes in v7:
time: 162 us; the launch traced here: 161 us
  blocking collectives  141 us (87%)
  Pallas kernels  19.3 us (12%)
    all_to_all x2, blocking collectives, exchange(): wire = lax.all_to_all(wire, ORDER, split_axis=0, concat_axis=0, tiled=True)  141 us
    pallas_call x1, Pallas kernels, body(): pl.pallas_call(ffn_kernel, out_shape=chunks, in_specs=[vmem] * 4, out_spe...  13.2 us
    pallas_call x1, Pallas kernels, body(): pl.pallas_call(functools.partial(dispatch_kernel, slots), out_shape=(chun...  3.49 us

profile of v7, /device:TPU:3, one launch (start us, length us, event | category | flops | bytes accessed | tf_op | source)
XLA Modules:
  0.0 160.7 jit_solution(2485457552942309279)
XLA Ops:
  0.0 3.5 %dispatch.1 = (bf16[128,20,8,128]{3,2,1,0:T(8,128)(2,1)S(1)}, bf16[256,1280]{1,0:T(8,128)(2,1)S(1)}) custom-call(s32[8,128]{1,0:T(8,128)} %bitcast.16, f32[8,128]{1,0:T(8,128)} %bitcast.17, bf16[128,2048]{1,0:T(8,128)(2,1)} %tok_hbm.1), custom_call_target="tpu_custom_call" | custom-call | tf_op jit(solution)/shard_map/dispatch/pallas_call | solution.py:206
  3.5 0.0 copy-start
  3.5 0.0 copy-start.1
  3.5 0.0 copy-start.2
  3.5 73.0 %all_to_all.10 = bf16[128,160,128]{2,1,0:T(8,128)(2,1)S(1)} all-to-all(bf16[128,160,128]{2,1,0:T(8,128)(2,1)S(1)} %bitcast.12), channel_id=1, replica_groups=mesh['zh'=2,'x'=4,'zl'=2,'y'=4,'core'=2] {'zl','y','core','x','zh'}, dimensions={0} | all-to-all | bytes 10485760 | tf_op jit(solution)/shard_map/all_to_all | solution.py:203
  76.5 0.0 copy-done
  76.5 0.0 copy-done.1
  76.5 0.0 copy-done.2
  76.6 13.2 %ffn.1 = bf16[128,20,8,128]{3,2,1,0:T(8,128)(2,1)S(1)} custom-call(bf16[128,20,8,128]{3,2,1,0:T(8,128)(2,1)S(1)} %bitcast.10, bf16[2048,768]{1,0:T(8,128)(2,1)S(1)} %bitcast.13, bf16[2048,768]{1,0:T(8,128)(2,1)S(1)} %bitcast.14, bf16[768,2048]{1,0:T(8,128)(2,1)S(1)} %bitcast.15), custom_call_target="tpu_custom_call" | custom-call | tf_op jit(solution)/shard_map/ffn/pallas_call | solution.py:222
  89.7 68.2 %all_to_all.11 = bf16[128,160,128]{2,1,0:T(8,128)(2,1)S(1)} all-to-all(bf16[128,160,128]{2,1,0:T(8,128)(2,1)S(1)} %bitcast.11), channel_id=1, replica_groups=mesh['zh'=2,'x'=4,'zl'=2,'y'=4,'core'=2] {'zl','y','core','x','zh'}, dimensions={0} | all-to-all | bytes 10485760 | tf_op jit(solution)/shard_map/all_to_all | solution.py:203
  157.9 2.6 %combine.1 = bf16[128,2048]{1,0:T(8,128)(2,1)} custom-call(bf16[256,1280]{1,0:T(8,128)(2,1)S(1)} %get-tuple-element.7.mix_ref, bf16[128,20,8,128]{3,2,1,0:T(8,128)(2,1)S(1)} %bitcast.9), custom_call_target="tpu_custom_call" | custom-call | tf_op jit(solution)/shard_map/combine/pallas_call | solution.py:232
Async XLA Ops:
  3.5 73.0 %copy-start = (bf16[1,2048,768]{2,1,0:T(8,128)(2,1)S(1)}, bf16[1,2048,768]{2,1,0:T(8,128)(2,1)}, u32[]{:S(2)}) copy-start(bf16[1,2048,768]{2,1,0:T(8,128)(2,1)} %param.9) | copy-start | bytes 9437188
  3.5 73.0 %copy-start.1 = (bf16[1,2048,768]{2,1,0:T(8,128)(2,1)S(1)}, bf16[1,2048,768]{2,1,0:T(8,128)(2,1)}, u32[]{:S(2)}) copy-start(bf16[1,2048,768]{2,1,0:T(8,128)(2,1)} %param.10) | copy-start | bytes 9437188
  3.5 73.0 %copy-start.2 = (bf16[1,768,2048]{2,1,0:T(8,128)(2,1)S(1)}, bf16[1,768,2048]{2,1,0:T(8,128)(2,1)}, u32[]{:S(2)}) copy-start(bf16[1,768,2048]{2,1,0:T(8,128)(2,1)} %param.11) | copy-start | bytes 9437188

commit v8 on v7

--- a/solution.py
+++ b/solution.py
@@ -145,8 +145,13 @@
     hidden = jnp.concatenate(parts, axis=1)
     for n in range(SUB // 2):
         cols = slice(n * 256, (n + 1) * 256)
-        store_columns(jnp.dot(hidden, wd_ref[:, cols], preferred_element_type=F32).astype(BF), n, out_ref, tail_ref)
+        tail_ref[:, cols] = jnp.dot(hidden[main:], wd_ref[:, cols], preferred_element_type=F32).astype(BF)
     store_pairs(tail_ref, out_ref)
+    for n in range(SUB // 2):
+        cols = slice(n * 256, (n + 1) * 256)
+        result = jnp.dot(hidden[:main], wd_ref[:, cols], preferred_element_type=F32).astype(BF)
+        for h in range(2):
+            out_ref[:, 2 * n + h] = result[:, h * LANES : (h + 1) * LANES].reshape(main // 8, 8, LANES)
 
 
 def combine_kernel(mix_ref, x_ref, out_hbm, tail_ref, out_ref, sems):

time: 162 us -> 162 us (level)
  no operation moved by 1% of the time
where the time goes in v8:
time: 162 us; the launch traced here: 161 us
  blocking collectives  141 us (87%)
  Pallas kernels  19.3 us (12%)
    all_to_all x2, blocking collectives, exchange(): wire = lax.all_to_all(wire, ORDER, split_axis=0, concat_axis=0, tiled=True)  141 us
    pallas_call x1, Pallas kernels, body(): pl.pallas_call(ffn_kernel, out_shape=chunks, in_specs=[vmem] * 4, out_spe...  13.2 us
    pallas_call x1, Pallas kernels, body(): pl.pallas_call(functools.partial(dispatch_kernel, slots), out_shape=(chun...  3.49 us

profile of v8, /device:TPU:3, one launch (start us, length us, event | category | flops | bytes accessed | tf_op | source)
XLA Modules:
  0.0 160.7 jit_solution(4768939774312277841)
XLA Ops:
  0.0 3.5 %dispatch.1 = (bf16[128,20,8,128]{3,2,1,0:T(8,128)(2,1)S(1)}, bf16[256,1280]{1,0:T(8,128)(2,1)S(1)}) custom-call(s32[8,128]{1,0:T(8,128)} %bitcast.16, f32[8,128]{1,0:T(8,128)} %bitcast.17, bf16[128,2048]{1,0:T(8,128)(2,1)} %tok_hbm.1), custom_call_target="tpu_custom_call" | custom-call | tf_op jit(solution)/shard_map/dispatch/pallas_call | solution.py:211
  3.5 0.0 copy-start
  3.5 0.0 copy-start.1
  3.5 0.0 copy-start.2
  3.5 73.0 %all_to_all.10 = bf16[128,160,128]{2,1,0:T(8,128)(2,1)S(1)} all-to-all(bf16[128,160,128]{2,1,0:T(8,128)(2,1)S(1)} %bitcast.12), channel_id=1, replica_groups=mesh['zh'=2,'x'=4,'zl'=2,'y'=4,'core'=2] {'zl','y','core','x','zh'}, dimensions={0} | all-to-all | bytes 10485760 | tf_op jit(solution)/shard_map/all_to_all | solution.py:208
  76.5 0.0 copy-done
  76.5 0.0 copy-done.1
  76.5 0.0 copy-done.2
  76.6 13.2 %ffn.1 = bf16[128,20,8,128]{3,2,1,0:T(8,128)(2,1)S(1)} custom-call(bf16[128,20,8,128]{3,2,1,0:T(8,128)(2,1)S(1)} %bitcast.10, bf16[2048,768]{1,0:T(8,128)(2,1)S(1)} %bitcast.13, bf16[2048,768]{1,0:T(8,128)(2,1)S(1)} %bitcast.14, bf16[768,2048]{1,0:T(8,128)(2,1)S(1)} %bitcast.15), custom_call_target="tpu_custom_call" | custom-call | tf_op jit(solution)/shard_map/ffn/pallas_call | solution.py:227
  89.7 68.2 %all_to_all.11 = bf16[128,160,128]{2,1,0:T(8,128)(2,1)S(1)} all-to-all(bf16[128,160,128]{2,1,0:T(8,128)(2,1)S(1)} %bitcast.11), channel_id=1, replica_groups=mesh['zh'=2,'x'=4,'zl'=2,'y'=4,'core'=2] {'zl','y','core','x','zh'}, dimensions={0} | all-to-all | bytes 10485760 | tf_op jit(solution)/shard_map/all_to_all | solution.py:208
  158.0 2.6 %combine.1 = bf16[128,2048]{1,0:T(8,128)(2,1)} custom-call(bf16[256,1280]{1,0:T(8,128)(2,1)S(1)} %get-tuple-element.7.mix_ref, bf16[128,20,8,128]{3,2,1,0:T(8,128)(2,1)S(1)} %bitcast.9), custom_call_target="tpu_custom_call" | custom-call | tf_op jit(solution)/shard_map/combine/pallas_call | solution.py:237
Async XLA Ops:
  3.5 73.0 %copy-start = (bf16[1,2048,768]{2,1,0:T(8,128)(2,1)S(1)}, bf16[1,2048,768]{2,1,0:T(8,128)(2,1)}, u32[]{:S(2)}) copy-start(bf16[1,2048,768]{2,1,0:T(8,128)(2,1)} %param.9) | copy-start | bytes 9437188
  3.5 73.0 %copy-start.1 = (bf16[1,2048,768]{2,1,0:T(8,128)(2,1)S(1)}, bf16[1,2048,768]{2,1,0:T(8,128)(2,1)}, u32[]{:S(2)}) copy-start(bf16[1,2048,768]{2,1,0:T(8,128)(2,1)} %param.10) | copy-start | bytes 9437188
  3.5 73.0 %copy-start.2 = (bf16[1,768,2048]{2,1,0:T(8,128)(2,1)S(1)}, bf16[1,768,2048]{2,1,0:T(8,128)(2,1)}, u32[]{:S(2)}) copy-start(bf16[1,768,2048]{2,1,0:T(8,128)(2,1)} %param.11) | copy-start | bytes 9437188
